TPU v7x, 32 devices: a whole 2x2x4 slice. The times are simulated.
32 devices in a mesh: keys: 8 (over z, y), view: 4 (over x, core).
Axes of the slice: x: 2, y: 2, z: 4, core: 2. Of those that a mesh axis runs over, the one named last changes fastest.
Arguments:
- key_slot: int32 [4096], replicated, may hold values from 0 to 4095, as said below
- a_slot: int32 [131072], P(('keys', 'view')), may hold values from 0 to 511
- a_group: int32 [131072], P(('keys', 'view')), may hold values from 0 to 1023
- a_weight: int32 [131072], P(('keys', 'view')), may hold values from 1 to 3
- a_payload: bfloat16 [131072, 256], P(('keys', 'view')), may hold values from -1.1953125 to 1.1953125
- b_slot: int32 [131072], P(('keys', 'view')), may hold values from 0 to 511
- b_weight: int32 [131072], P(('keys', 'view')), may hold values from 1 to 3
- b_payload: bfloat16 [131072, 256], P(('keys', 'view')), may hold values from -0.59765625 to 0.59765625
- da_key: int32 [32768], P(('keys', 'view')), may hold values from 0 to 4095, as said below
- da_group: int32 [32768], P(('keys', 'view')), may hold values from 0 to 1023
- da_mult: int32 [32768], P(('keys', 'view')), may hold values from -1 to 1, as said below
- da_payload: bfloat16 [32768, 256], P(('keys', 'view')), may hold values from -1.796875 to 1.796875
- da_count: int32 [32], P(('keys', 'view')), may hold values from 768 to 1024, as said below
- db_key: int32 [32768], P(('keys', 'view')), may hold values from 0 to 4095, as said below
- db_mult: int32 [32768], P(('keys', 'view')), may hold values from -1 to 1, as said below
- db_payload: bfloat16 [32768, 256], P(('keys', 'view')), may hold values from -1.1953125 to 1.1953125
- db_count: int32 [32], P(('keys', 'view')), may hold values from 768 to 1024, as said below
Outputs:
- view_delta: float32 [1024, 256], P(('keys', 'view'))
Inputs may be any that keep to these rules, and one draw needn't show every extreme that they name: `key_slot`: A permutation of 0 to 4095. `da_key`: among the 1024 slots of one device, at most 256 have keys held by one keys index; in every draw one keys index gets exactly 256 live rows from every device. `db_key`: among the 1024 slots of one device, at most 256 have keys held by one keys index; in every draw one keys index gets exactly 256 live rows from every device. `da_mult`: each entry is -1 or 1. `db_mult`: each entry is -1 or 1. `da_count`: some device has all 1024 rows live. `db_count`: some device has all 1024 rows live.
All inputs are finite; a program needn't handle non-finite values.
Results may differ from a plain program's by a relative error of at most 0.0029.
Values may be sent and summed in bfloat16 or wider, within the bound.
A program may use at most 64 MiB of HBM per device.

v0:
```python
import jax
import jax.numpy as jnp
from jax import lax
from jax.sharding import PartitionSpec as P

KEYS_DEV = 512
GROUPS_DEV = 32
DELTA_DEV = 1024


def pack_rows(key_slot, row_keys, row_mult, row_count, payload, extra_columns, owners):
    capacity = 2 * DELTA_DEV // owners
    alive_rows = jnp.arange(DELTA_DEV, dtype=jnp.int32) < row_count[0]
    slots = jnp.take(key_slot, row_keys)
    target = slots // KEYS_DEV
    marks = (target[:, None] == jnp.arange(owners, dtype=jnp.int32)[None, :]).astype(
        jnp.int32
    ) * alive_rows[:, None].astype(jnp.int32)
    before = jnp.cumsum(marks, axis=0) - marks
    slot_rank = jnp.take_along_axis(before, target[:, None], axis=1)[:, 0]
    position = jnp.where(alive_rows, target * capacity + slot_rank, owners * capacity)
    columns = jnp.stack(
        [slots % KEYS_DEV, row_mult * alive_rows.astype(jnp.int32)] + extra_columns, axis=1
    )
    sent_payload = (
        jnp.zeros((owners * capacity + 1, payload.shape[1]), payload.dtype)
        .at[position]
        .set(payload)
    )
    sent_columns = (
        jnp.zeros((owners * capacity + 1, columns.shape[1]), jnp.int32).at[position].set(columns)
    )
    return (
        sent_payload[:-1].reshape(owners, capacity, payload.shape[1]),
        sent_columns[:-1].reshape(owners, capacity, columns.shape[1]),
    )


def shards(
    key_slot,
    a_slot,
    a_group,
    a_weight,
    a_payload,
    b_slot,
    b_weight,
    b_payload,
    da_key,
    da_group,
    da_mult,
    da_payload,
    da_count,
    db_key,
    db_mult,
    db_payload,
    db_count,
):
    owners = lax.axis_size("keys")
    width = a_payload.shape[1]
    a_sent, a_columns = pack_rows(
        key_slot, da_key, da_mult, da_count, da_payload, [da_group], owners
    )
    a_payload_in, a_columns_in = (
        lax.all_to_all(a_sent, "keys", split_axis=0, concat_axis=0, tiled=True),
        lax.all_to_all(a_columns, "keys", split_axis=0, concat_axis=0, tiled=True),
    )
    weighted_b = b_weight[:, None].astype(jnp.float32) * b_payload.astype(jnp.float32)
    local_b = jax.ops.segment_sum(weighted_b, b_slot, num_segments=KEYS_DEV)
    b_sent, b_columns = pack_rows(key_slot, db_key, db_mult, db_count, db_payload, [], owners)
    b_payload_in, b_columns_in = (
        lax.all_to_all(b_sent, "keys", split_axis=0, concat_axis=0, tiled=True),
        lax.all_to_all(b_columns, "keys", split_axis=0, concat_axis=0, tiled=True),
    )
    flat_columns = b_columns_in.reshape(-1, 2)
    terms = flat_columns[:, 1:2].astype(jnp.float32) * b_payload_in.reshape(-1, width).astype(
        jnp.float32
    )
    local_db = jax.ops.segment_sum(terms, flat_columns[:, 0], num_segments=KEYS_DEV)
    total_b, total_db = lax.psum((local_b, local_db), "view")
    whole_table = total_b + total_db
    a_terms = (
        a_weight[:, None].astype(jnp.float32)
        * a_payload.astype(jnp.float32)
        * jnp.take(total_db, a_slot, axis=0)
    ).astype(jnp.bfloat16)
    delta_columns = a_columns_in.reshape(-1, 3)
    delta_terms = (
        delta_columns[:, 1:2].astype(jnp.float32)
        * a_payload_in.reshape(-1, width).astype(jnp.float32)
        * jnp.take(whole_table, delta_columns[:, 0], axis=0)
    ).astype(jnp.bfloat16)
    all_terms = jnp.concatenate([a_terms, delta_terms], axis=0)
    all_groups = jnp.concatenate([a_group, delta_columns[:, 2]])
    row_total = GROUPS_DEV * lax.axis_size(("keys", "view"))
    shifted = all_groups - jnp.int32(0)
    inside = (shifted >= 0) & (shifted < row_total)
    segment_index = jnp.where(inside, shifted, row_total)
    summed = jax.ops.segment_sum(
        all_terms.astype(jnp.float32), segment_index, num_segments=row_total + 1
    )
    return lax.psum_scatter(summed[:row_total], ("keys", "view"), scatter_dimension=0, tiled=True)


def solution(mesh):
    in_specs = (
        P(),
        P(("keys", "view")),
        P(("keys", "view")),
        P(("keys", "view")),
        P(("keys", "view"), None),
        P(("keys", "view")),
        P(("keys", "view")),
        P(("keys", "view"), None),
        P(("keys", "view")),
        P(("keys", "view")),
        P(("keys", "view")),
        P(("keys", "view"), None),
        P(("keys", "view")),
        P(("keys", "view")),
        P(("keys", "view")),
        P(("keys", "view"), None),
        P(("keys", "view")),
    )
    out_specs = P(("keys", "view"), None)
    return jax.shard_map(shards, mesh=mesh, in_specs=in_specs, out_specs=out_specs, check_vma=False)
```

profile of v0, /device:TPU:0, one launch (start us, length us, event | category | flops | bytes accessed | tf_op | source)
XLA Modules:
  0.0 382.8 jit_solution(13308188661534247323)
XLA Ops:
  7.3 6.2 %gather_fusion.4 = s32[1024]{0:T(1024)S(1)} fusion(s32[4096]{0:T(1024)S(1)} %copy-done, s32[1024]{0:T(1024)S(1)} %fusion.48), kind=kCustom, calls=%fused_computation.2.clone | custom fusion | bytes 12288 | tf_op jit(solution)/shard_map/jit(_take)/gather | solution.py:14
  14.1 2.3 reduce-window.16
  17.0 6.2 %gather_fusion.2 = s32[1024]{0:T(1024)S(1)} fusion(s32[4096]{0:T(1024)S(1)} %copy-done, s32[1024]{0:T(1024)S(1)} %fusion.47), kind=kCustom, calls=%fused_computation.clone | custom fusion | bytes 12288 | tf_op jit(solution)/shard_map/jit(_take)/gather | solution.py:14
  23.3 6.5 %gather_fusion.5 = s32[1024]{0:T(1024)S(1)} fusion(s32[1024,8]{0,1:T(8,128)S(1)} %fusion.24, s32[1024]{0:T(1024)S(1)} %bitcast.70), kind=kCustom, calls=%fused_computation.3.clone | custom fusion | bytes 16384 | tf_op jit(solution)/shard_map/jit(take_along_axis)/gather | solution.py:20
  30.1 3.3 scatter_custom_fusion.1
  34.4 7.3 %all-to-all-start.1 = ((s32[8,256,2]{1,2,0:T(2,128)}), s32[8,256,2]{1,2,0:T(2,128)S(1)}, u32[]{:S(2)}, u32[]{:S(2)}) async-start(s32[8,256,2]{1,2,0:T(2,128)} %copy.25), calls=%async_computation.1 | async-start | bytes 32768 | tf_op jit(solution)/shard_map/all_to_all | solution.py:72
  42.4 2.3 reduce-window.14
  45.3 6.5 %gather_fusion.3 = s32[1024]{0:T(1024)S(1)} fusion(s32[1024,8]{0,1:T(8,128)S(1)} %fusion.25, s32[1024]{0:T(1024)S(1)} %bitcast.71), kind=kCustom, calls=%fused_computation.1.clone | custom fusion | bytes 16384 | tf_op jit(solution)/shard_map/jit(take_along_axis)/gather | solution.py:20
  52.1 3.3 scatter_custom_fusion
  56.5 6.0 %all-to-all-start = ((s32[8,256,3]{1,2,0:T(4,128)}), s32[8,256,3]{1,2,0:T(4,128)S(1)}, u32[]{:S(2)}, u32[]{:S(2)}) async-start(s32[8,256,3]{1,2,0:T(4,128)} %copy.23), calls=%async_computation | async-start | bytes 65536 | tf_op jit(solution)/shard_map/all_to_all | solution.py:65
  62.5 5.6 %scatter_custom_fusion.2 = bf16[2049,256]{1,0:T(8,128)(2,1)S(1)} fusion(s32[1024]{0:T(1024)S(1)} %get-tuple-element.23, bf16[1024,256]{1,0:T(8,128)(2,1)} %param.36, bf16[]{:T(256)} %constant.112.clone.1), kind=kCustom, calls=%fused_computation.32 | custom fusion | bytes 1049600 | tf_op jit(solution)/shard_map/scatter | solution.py:28
  69.2 6.0 %all-to-all-start.2 = ((bf16[8,256,256]{2,1,0:T(8,128)(2,1)}), bf16[8,256,256]{2,1,0:T(8,128)(2,1)S(1)}, u32[]{:S(2)}, u32[]{:S(2)}) async-start(bf16[8,256,256]{2,1,0:T(8,128)(2,1)} %bitcast.31), calls=%async_computation.2 | async-start | bytes 2097152 | tf_op jit(solution)/shard_map/all_to_all | solution.py:71
  75.2 5.8 %scatter_custom_fusion.4 = bf16[2049,256]{1,0:T(8,128)(2,1)S(1)} fusion(s32[1024]{0:T(1024)S(1)} %get-tuple-element.21, bf16[1024,256]{1,0:T(8,128)(2,1)} %param.32, bf16[]{:T(256)} %constant.112.clone.1), kind=kCustom, calls=%fused_computation.30 | custom fusion | bytes 1049600 | tf_op jit(solution)/shard_map/scatter | solution.py:28
  81.1 1.1 slice.85
  82.2 25.7 %scatter_custom_fusion.5 = f32[512,256]{1,0:T(8,128)} fusion(s32[4096]{0:T(1024)} %param.26, bf16[4096,256]{1,0:T(8,128)(2,1)} %param.28, f32[4096]{0:T(1024)S(1)} %convert_element_type.80, f32[]{:T(128)} %constant.100.clone.1), kind=kCustom, calls=%fused_computation.15 | custom fusion | flops 3145728 | bytes 2638336 | tf_op jit(solution)/shard_map/scatter-add | solution.py:68
  108.0 6.0 %all-to-all-start.3 = ((bf16[8,256,256]{2,1,0:T(8,128)(2,1)}), bf16[8,256,256]{2,1,0:T(8,128)(2,1)}, u32[]{:S(2)}, u32[]{:S(2)}) async-start(bf16[8,256,256]{2,1,0:T(8,128)(2,1)} %bitcast.34), calls=%async_computation.3 | async-start | bytes 2097152 | tf_op jit(solution)/shard_map/all_to_all | solution.py:64
  114.0 15.2 %scatter_custom_fusion.3 = f32[512,256]{1,0:T(8,128)} fusion(s32[2048]{0:T(1024)S(1)} %bitcast.99, bf16[2048,256]{1,0:T(8,128)(2,1)S(1)} %bitcast.72, f32[2048]{0:T(1024)S(1)} %bitcast.85, f32[]{:T(128)} %constant.100.clone.1), kind=kCustom, calls=%fused_computation.26 | custom fusion | flops 1572864 | bytes 1581060 | tf_op jit(solution)/shard_map/scatter-add | solution.py:78
  129.4 37.8 %all-reduce.3.cloned.1.call-done = (f32[512,256]{1,0:T(8,128)}, f32[512,256]{1,0:T(8,128)}) async-done(((f32[512,256]{1,0:T(8,128)}, f32[512,256]{1,0:T(8,128)}), (f32[512,256]{1,0:T(8,128)}, f32[512,256]{1,0:T(8,128)})) %all-reduce.3.cloned.1.call-update) | async-done | bytes 1048592 | tf_op jit(solution)/shard_map/psum | solution.py:79
  167.2 17.2 %gather_fusion = f32[4096,256]{1,0:T(8,128)} fusion(f32[512,256]{1,0:T(8,128)} %get-tuple-element.8, s32[4096]{0:T(1024)S(1)} %fusion.28), kind=kCustom, calls=%fused_computation.4 | custom fusion | bytes 8404992 | tf_op jit(solution)/shard_map/jit(_take)/gather | solution.py:84
  184.5 6.6 %gather_fusion.1 = f32[2048,256]{1,0:T(8,128)S(1)} fusion(f32[512,256]{1,0:T(8,128)S(1)} %add.83, s32[2048]{0:T(1024)S(1)} %broadcast_clamp_fusion), kind=kCustom, calls=%fused_computation.5 | custom fusion | bytes 4202496 | tf_op jit(solution)/shard_map/jit(_take)/gather | solution.py:90
  191.1 5.9 %multiply_convert_fusion = bf16[4096,256]{1,0:T(8,128)(2,1)} fusion(f32[4096,256]{1,0:T(8,128)} %gather_fusion, bf16[4096,256]{1,0:T(8,128)(2,1)} %param.25, f32[4096]{0:T(1024)S(1)} %convert_element_type.69, pred[4096]{0:T(1024)(128)(4,1)S(1)} %compare_and_fusion), kind=kLoop, calls=%fused_computation.18 | loop fusion | flops 5242880 | bytes 8409088 | tf_op jit(solution)/shard_map/convert_element_type | solution.py:85
  197.0 1.8 fusion.9
  198.8 37.0 %scatter_custom_fusion.6 = f32[1025,256]{1,0:T(8,128)S(1)} fusion(s32[6144]{0:T(1024)S(1)} %bitcast.87, bf16[2048,256]{1,0:T(8,128)(2,1)S(1)} %fusion.9, bf16[]{:T(256)} %constant.157, bf16[4096,256]{1,0:T(8,128)(2,1)} %multiply_convert_fusion, f32[]{:T(128)} %constant.100.clone.1), kind=kCustom, calls=%fused_computation.13 | custom fusion | flops 7864320 | bytes 4195334 | tf_op jit(solution)/shard_map/scatter-add | solution.py:98
  236.9 139.0 %reduce-scatter.2.cloned.1.call-done = f32[32,256]{1,0:T(8,128)} async-done(((f32[1024,256]{1,0:T(8,128)}), f32[32,256]{1,0:T(8,128)}) %reduce-scatter.2.cloned.1.call-update) | async-done | bytes 32784 | tf_op jit(solution)/shard_map/reduce_scatter | solution.py:101
  (80 shorter events, 7.0 us)
Async XLA Ops:
  6.5 0.7 copy-start
  7.3 6.2 %copy-start.7 = (s32[1024]{0:T(1024)S(1)}, s32[1024]{0:T(1024)}, u32[]{:S(2)}) copy-start(s32[1024]{0:T(1024)} %param.34) | copy-start | bytes 12292
  7.3 9.7 %copy-start.8 = (s32[1024]{0:T(1024)S(1)}, s32[1024]{0:T(1024)}, u32[]{:S(2)}) copy-start(s32[1024]{0:T(1024)} %param.29) | copy-start | bytes 12292
  23.3 6.6 %copy-start.10 = (s32[1024]{0:T(1024)S(1)}, s32[1024]{0:T(1024)}, u32[]{:S(2)}) copy-start(s32[1024]{0:T(1024)} %param.35) | copy-start | bytes 12292
  34.4 22.1 %all-to-all-start.1 = ((s32[8,256,2]{1,2,0:T(2,128)}), s32[8,256,2]{1,2,0:T(2,128)S(1)}, u32[]{:S(2)}, u32[]{:S(2)}) async-start(s32[8,256,2]{1,2,0:T(2,128)} %copy.25), calls=%async_computation.1 | async-start | bytes 32768 | tf_op jit(solution)/shard_map/all_to_all | solution.py:72
  45.3 6.6 %copy-start.11 = (s32[1024]{0:T(1024)S(1)}, s32[1024]{0:T(1024)}, u32[]{:S(2)}) copy-start(s32[1024]{0:T(1024)} %param.31) | copy-start | bytes 12292
  45.3 6.6 %copy-start.9 = (s32[1024]{0:T(1024)S(1)}, s32[1024]{0:T(1024)}, u32[]{:S(2)}) copy-start(s32[1024]{0:T(1024)} %param.30) | copy-start | bytes 12292
  56.5 12.7 %all-to-all-start = ((s32[8,256,3]{1,2,0:T(4,128)}), s32[8,256,3]{1,2,0:T(4,128)S(1)}, u32[]{:S(2)}, u32[]{:S(2)}) async-start(s32[8,256,3]{1,2,0:T(4,128)} %copy.23), calls=%async_computation | async-start | bytes 65536 | tf_op jit(solution)/shard_map/all_to_all | solution.py:65
  68.1 7.1 %copy-start.5 = (s32[4096]{0:T(1024)S(1)}, s32[4096]{0:T(1024)}, u32[]{:S(2)}) copy-start(s32[4096]{0:T(1024)} %param.27) | copy-start | bytes 49156
  68.1 7.1 %copy-start.6 = (s32[4096]{0:T(1024)S(1)}, s32[4096]{0:T(1024)}, u32[]{:S(2)}) copy-start(s32[4096]{0:T(1024)} %param.24) | copy-start | bytes 49156
  69.2 38.7 %all-to-all-start.2 = ((bf16[8,256,256]{2,1,0:T(8,128)(2,1)}), bf16[8,256,256]{2,1,0:T(8,128)(2,1)S(1)}, u32[]{:S(2)}, u32[]{:S(2)}) async-start(bf16[8,256,256]{2,1,0:T(8,128)(2,1)} %bitcast.31), calls=%async_computation.2 | async-start | bytes 2097152 | tf_op jit(solution)/shard_map/all_to_all | solution.py:71
  81.1 26.7 %copy-start.3 = (s32[4096]{0:T(1024)S(1)}, s32[4096]{0:T(1024)}, u32[]{:S(2)}) copy-start(s32[4096]{0:T(1024)} %param.22) | copy-start | bytes 49156
  108.0 21.3 %copy-start.4 = (s32[4096]{0:T(1024)S(1)}, s32[4096]{0:T(1024)}, u32[]{:S(2)}) copy-start(s32[4096]{0:T(1024)} %param.23) | copy-start | bytes 49156
  108.0 89.0 %all-to-all-start.3 = ((bf16[8,256,256]{2,1,0:T(8,128)(2,1)}), bf16[8,256,256]{2,1,0:T(8,128)(2,1)}, u32[]{:S(2)}, u32[]{:S(2)}) async-start(bf16[8,256,256]{2,1,0:T(8,128)(2,1)} %bitcast.34), calls=%async_computation.3 | async-start | bytes 2097152 | tf_op jit(solution)/shard_map/all_to_all | solution.py:64
  114.0 53.2 %all-reduce.3.cloned.1.call-start = ((), (), s32[]{:S(2)}) async-start(), calls=%async_computation.6 | async-start | bytes 2097152 | tf_op jit(solution)/shard_map/psum | solution.py:79
  129.2 246.7 %reduce-scatter.2.cloned.1.call-start = ((), (), s32[]{:S(2)}) async-start(), calls=%async_computation.5 | async-start | bytes 1081344 | tf_op jit(solution)/shard_map/reduce_scatter | solution.py:101
  167.2 17.2 %copy-start.1 = (f32[512,256]{1,0:T(8,128)S(1)}, f32[512,256]{1,0:T(8,128)}, u32[]{:S(2)}) copy-start(f32[512,256]{1,0:T(8,128)} %get-tuple-element.8) | copy-start | bytes 1572868
  167.2 17.2 %copy-start.2 = (f32[512,256]{1,0:T(8,128)S(1)}, f32[512,256]{1,0:T(8,128)}, u32[]{:S(2)}) copy-start(f32[512,256]{1,0:T(8,128)} %get-tuple-element.6) | copy-start | bytes 1572868
Sparse Core Ops, SparseCore 0:
  129.4 37.7 all-reduce.2
  237.0 138.8 reduce-scatter.1
where the time goes:
time: 383 us
  waiting for transfers between devices  177 us (46%)
  other arithmetic  91.7 us (24%)
  local copies, waits for them, and re-layouts  73.6 us (19%)
  starting transfers between devices  25.4 us (7%)
  between operations  15.2 us (4%)
    reduce_scatter x1, waiting for transfers between devices, shards(): lax.psum_scatter(summed[:row_total], ('keys', 'view'), scatter_dimension=...  139 us
    psum x1, waiting for transfers between devices, shards(): total_b, total_db = lax.psum((local_b, local_db), 'view')  37.8 us
    scatter-add x1, other arithmetic, shards(): jax.ops.segment_sum(all_terms.astype(jnp.float32), segment_index, num_seg...  37 us
    scatter-add x1, other arithmetic, shards(): local_b = jax.ops.segment_sum(weighted_b, b_slot, num_segments=KEYS_DEV)  25.7 us
    gather x1, local copies, waits for them, and re-layouts, shards(): jnp.take(total_db, a_slot, axis=0)  17.2 us
    scatter-add x1, other arithmetic, shards(): jax.ops.segment_sum(terms, flat_columns[:, 0], num_segments=KEYS_DEV)  15.2 us
    gather x2, local copies, waits for them, and re-layouts, pack_rows(): slot_rank = jnp.take_along_axis(before, target[:, None], axis=1)[:, 0]  13 us
    gather x2, local copies, waits for them, and re-layouts, pack_rows(): slots = jnp.take(key_slot, row_keys)  12.3 us
  transfers between devices with their start and end apart: 6, of which 2 were waited for; matrix products, arithmetic and copies ran while one was open for 26% of the time, Pallas kernels for 0%

commit v1 on v0

v1 whole, which is shorter than its diff:
```python
import functools

import jax
import jax.numpy as jnp
from jax import lax
from jax.experimental import pallas as pl
from jax.experimental.pallas import tpu as pltpu
from jax.sharding import PartitionSpec as P

LANES = 128
META = 16
F32 = jnp.float32
BF16 = jnp.bfloat16
VMEM_LIMIT = 60 * 1024 * 1024


def row_of(ref, start, count):
    return jnp.concatenate([ref[pl.ds(start + i, 1), :] for i in range(count)], axis=1)


def as_row(ref):
    return row_of(ref, 0, ref.shape[0])


def iota(shape, axis):
    return lax.broadcasted_iota(jnp.int32, shape, axis)


def dot(a, b):
    return jnp.dot(a, b, preferred_element_type=F32)


def pack_side(owners, keys_dev, cap, base, table_ref, key_ref, mult_ref, group_ref, count, pay_ref, out_ref):
    rows = pay_ref.shape[0]
    tiles = table_ref.shape[0]
    key = as_row(key_ref)
    table = table_ref[...]
    halves = jnp.concatenate([table & 255, table >> 8], axis=0).astype(F32).astype(BF16)
    low = jnp.where(iota((LANES, rows), 0) == (key & (LANES - 1)), 1.0, 0.0).astype(BF16)
    looked = dot(halves, low)
    high = iota((tiles, rows), 0) == (key >> 7)
    slot_low = jnp.sum(jnp.where(high, looked[:tiles], 0.0), axis=0, keepdims=True)
    slot_high = jnp.sum(jnp.where(high, looked[tiles:], 0.0), axis=0, keepdims=True)
    slot = slot_low.astype(jnp.int32) + 256 * slot_high.astype(jnp.int32)
    owner = slot // keys_dev
    local = slot - owner * keys_dev
    alive = iota((1, rows), 1) < count
    marks = jnp.where((iota((owners, rows), 0) == owner) & alive, 1.0, 0.0)
    step = min(256, rows)
    upper = jnp.where(iota((step, step), 0) < iota((step, step), 1), 1.0, 0.0).astype(BF16)
    running = jnp.zeros((owners, 1), F32)
    ranks = []
    for at in range(0, rows, step):
        piece = marks[:, at:at + step]
        before = dot(piece.astype(BF16), upper) + running
        ranks.append(jnp.sum(piece * before, axis=0, keepdims=True))
        running = running + jnp.sum(piece, axis=1, keepdims=True)
    rank = jnp.concatenate(ranks, axis=1).astype(jnp.int32)
    dest = jnp.where(alive, owner * cap + rank, -1)
    sign = as_row(mult_ref).astype(F32)
    group = jnp.zeros((1, rows), jnp.int32) if group_ref is None else as_row(group_ref)
    parts = [local & 255, local >> 8, group & 255, group >> 8]
    meta = jnp.concatenate(
        [p.astype(F32) * sign for p in parts] + [jnp.zeros((META - 4, rows), F32)], axis=0
    ).astype(BF16)
    payload = pay_ref[...]

    def one(o, carry):
        place = jnp.where(iota((cap, rows), 0) == dest - o * cap, sign, 0.0).astype(BF16)
        out_ref[o, base:base + cap, :] = dot(place, payload).astype(BF16)
        columns = lax.dot_general(meta, place, (((1,), (1,)), ((), ())), preferred_element_type=F32)
        out_ref[o, base + cap:base + cap + META, :cap] = columns.astype(BF16)
        return carry

    lax.fori_loop(0, owners, one, 0)


def pack_kernel(owners, keys_dev, cap, a_count, b_count, table, a_key, a_group, a_mult, b_key, b_mult, a_pay, b_pay, out):
    pack_side(owners, keys_dev, cap, 0, table, a_key, a_mult, a_group, a_count[0], a_pay, out)
    pack_side(owners, keys_dev, cap, cap + META, table, b_key, b_mult, None, b_count[0], b_pay, out)


def meta_row(got, o, row, cap):
    low = got[o, row:row + 1, :cap].astype(F32)
    high = got[o, row + 1:row + 2, :cap].astype(F32)
    return low.astype(jnp.int32) + 256 * high.astype(jnp.int32)


def base_kernel(keys_dev, slot_ref, weight_ref, pay_ref, out_ref):
    chunk = min(1024, pay_ref.shape[0])
    lines = chunk // LANES
    out_ref[...] = jnp.zeros_like(out_ref)

    def one(c, carry):
        slot = row_of(slot_ref, c * lines, lines)
        weight = row_of(weight_ref, c * lines, lines).astype(F32)
        marks = jnp.where(iota((keys_dev, chunk), 0) == slot, weight, 0.0).astype(BF16)
        rows = pl.ds(pl.multiple_of(c * chunk, chunk), chunk)
        out_ref[...] += dot(marks, pay_ref[rows, :])
        return carry

    lax.fori_loop(0, pay_ref.shape[0] // chunk, one, 0)


def delta_kernel(keys_dev, cap, local_b, got, out_ref):
    base = cap + META
    width = local_b.shape[1]
    out_ref[:, :width] = local_b[...]
    out_ref[:, width:] = jnp.zeros_like(local_b)

    def one(o, carry):
        slot = meta_row(got, o, base + cap, cap)
        marks = jnp.where(iota((keys_dev, cap), 0) == slot, 1.0, 0.0).astype(BF16)
        out_ref[:, width:] += dot(marks, got[o, base:base + cap, :])
        return carry

    lax.fori_loop(0, got.shape[0], one, 0)


def split(x):
    top = x.astype(BF16)
    return jnp.concatenate([top, (x - top.astype(F32)).astype(BF16)], axis=1)


def columns_of(row, width):
    return jnp.transpose(jnp.broadcast_to(row, (width, row.shape[1])))


def gathered(row, weight, table, width):
    count, keys_dev = row.shape[1], table.shape[0]
    code = columns_of(row * 4 + weight, LANES)
    slot, scale = code >> 2, (code & 3).astype(F32)
    marks = jnp.concatenate(
        [
            jnp.where(iota((count, LANES), 1) + at == slot, scale, 0.0).astype(BF16)
            for at in range(0, keys_dev, LANES)
        ],
        axis=1,
    )
    both = dot(marks, table)
    return both[:, :width] + both[:, width:]


def terms_kernel(
    cap, a_slot, a_weight, a_group, a_pay, got, totals, out, a_table, d_table, a_terms, d_terms
):
    width = a_pay.shape[1]
    owners = got.shape[0]
    groups = out.shape[0]
    db = totals[:, width:]
    a_table[...] = split(db)
    d_table[...] = split(totals[:, :width] + db)
    chunk = min(256, a_pay.shape[0])
    lines = chunk // LANES

    def a_one(c, carry):
        rows = pl.ds(pl.multiple_of(c * chunk, chunk), chunk)
        picked = gathered(
            row_of(a_slot, c * lines, lines), row_of(a_weight, c * lines, lines), a_table[...], width
        )
        a_terms[rows, :] = (a_pay[rows, :].astype(F32) * picked).astype(BF16)
        return carry

    lax.fori_loop(0, a_pay.shape[0] // chunk, a_one, 0)

    def d_one(o, carry):
        slot = meta_row(got, o, cap, cap)
        picked = gathered(slot, jnp.ones_like(slot), d_table[...], width)
        d_terms[o] = (got[o, :cap, :].astype(F32) * picked).astype(BF16)
        return carry

    lax.fori_loop(0, owners, d_one, 0)

    block = min(256, groups)
    span = min(1024, a_pay.shape[0])
    span_lines = span // LANES

    def g_one(g, carry):
        first = g * block
        total = jnp.zeros((block, width), F32)
        ids = iota((block, 1), 0) + first
        for c in range(a_pay.shape[0] // span):
            group = row_of(a_group, c * span_lines, span_lines)
            marks = jnp.where(ids == group, 1.0, 0.0).astype(BF16)
            total = total + dot(marks, a_terms[c * span:(c + 1) * span, :])
        for o in range(owners):
            group = meta_row(got, o, cap + 2, cap)
            marks = jnp.where(ids == group, 1.0, 0.0).astype(BF16)
            total = total + dot(marks, d_terms[o])
        out[pl.ds(pl.multiple_of(first, block), block), :] = total.astype(BF16)
        return carry

    lax.fori_loop(0, groups // block, g_one, 0)


def call(body, shape, dtype, scratch=(), smem=0):
    def run(*args):
        specs = [pl.BlockSpec(memory_space=pltpu.SMEM)] * smem + [
            pl.BlockSpec(memory_space=pltpu.VMEM)
        ] * (len(args) - smem)
        return pl.pallas_call(
            body,
            out_shape=jax.ShapeDtypeStruct(shape, dtype),
            in_specs=specs,
            out_specs=pl.BlockSpec(memory_space=pltpu.VMEM),
            scratch_shapes=list(scratch),
            compiler_params=pltpu.CompilerParams(vmem_limit_bytes=VMEM_LIMIT),
        )(*args)

    return run


def view_total(x, views):
    me = lax.axis_index("view")
    trail = []
    bit = 1
    while bit < views:
        pairs = [(i, i ^ bit) for i in range(views)]
        if bit * 2 < views:
            mine = (me // bit) % 2
            half = x.shape[0] // 2
            keep = lax.dynamic_slice_in_dim(x, mine * half, half, 0)
            give = lax.dynamic_slice_in_dim(x, (1 - mine) * half, half, 0)
            x = keep + lax.ppermute(give, "view", pairs)
            trail.append((pairs, mine))
        else:
            x = x + lax.ppermute(x, "view", pairs)
        bit *= 2
    for pairs, mine in reversed(trail):
        other = lax.ppermute(x, "view", pairs)
        x = jnp.where(mine == 0, jnp.concatenate([x, other]), jnp.concatenate([other, x]))
    return x


def shards(
    keys_total, key_slot, a_slot, a_group, a_weight, a_payload, b_slot, b_weight, b_payload,
    da_key, da_group, da_mult, da_payload, da_count, db_key, db_mult, db_payload, db_count,
):
    owners, views = lax.axis_size("keys"), lax.axis_size("view")
    devices = owners * views
    width = a_payload.shape[1]
    keys_dev = key_slot.shape[0] // owners
    delta = da_payload.shape[0]
    cap = 2 * delta // owners
    groups = keys_total

    def lined(x):
        return x.reshape(-1, LANES)

    sent = call(
        functools.partial(pack_kernel, owners, keys_dev, cap), (owners, 2 * (cap + META), width), BF16, smem=2
    )(
        da_count, db_count, lined(key_slot), lined(da_key), lined(da_group), lined(da_mult),
        lined(db_key), lined(db_mult), da_payload, db_payload,
    )
    got = lax.all_to_all(sent, "keys", split_axis=0, concat_axis=0, tiled=True)
    local_b = call(functools.partial(base_kernel, keys_dev), (keys_dev, width), F32)(
        lined(b_slot), lined(b_weight), b_payload
    )
    local = call(functools.partial(delta_kernel, keys_dev, cap), (keys_dev, 2 * width), F32)(local_b, got)
    totals = view_total(local, views)
    summed = call(
        functools.partial(terms_kernel, cap),
        (groups, width),
        BF16,
        scratch=[
            pltpu.VMEM((keys_dev, 2 * width), BF16),
            pltpu.VMEM((keys_dev, 2 * width), BF16),
            pltpu.VMEM(a_payload.shape, BF16),
            pltpu.VMEM((owners, cap, width), BF16),
        ],
    )(
        lined(a_slot), lined(a_weight), lined(a_group), a_payload, got, totals
    )
    pieces = lax.all_to_all(
        summed.reshape(devices, groups // devices, width), ("keys", "view"), split_axis=0, concat_axis=0, tiled=True
    )
    return jnp.sum(pieces.astype(F32), axis=0)


GROUPS_DEV = 32


def solution(mesh):
    row, wide = P(("keys", "view")), P(("keys", "view"), None)
    groups = GROUPS_DEV * mesh.shape["keys"] * mesh.shape["view"]
    in_specs = (P(), row, row, row, wide, row, row, wide, row, row, row, wide, row, row, row, wide, row)
    return jax.shard_map(
        functools.partial(shards, groups), mesh=mesh, in_specs=in_specs, out_specs=wide, check_vma=False
    )
```

time: 383 us -> 134 us (0.35)
  waiting for transfers between devices: 177 us -> 63 us
  other arithmetic: 91.7 us -> 3 us
  local copies, waits for them, and re-layouts: 73.6 us -> 2.44 us
  Pallas kernels: 0 us -> 35.5 us
  blocking collectives: 0 us -> 19.3 us
  starting transfers between devices: 25.4 us -> 9.01 us
  between operations: 15.2 us -> 1.34 us
    reduce_scatter x1 -> x0, waiting for transfers between devices: 139 us -> none  [shards(): lax.psum_scatter(summed[:row_total], ('keys', 'view'), scatter_dimension=...]
    scatter-add x3 -> x0, other arithmetic: 77.9 us -> none  [the longest x1 37 us: shards(): jax.ops.segment_sum(all_terms.astype(jnp.float32), segment_index, num_seg...]
    gather x6 -> x0, local copies, waits for them, and re-layouts: 49.2 us -> none  [the longest x1 17.2 us: shards(): jnp.take(total_db, a_slot, axis=0)]
    all_to_all x4 -> x1, waiting for transfers between devices: 0.01 us -> 46.8 us  [shards(): got = lax.all_to_all(sent, 'keys', split_axis=0, concat_axis=0, tiled=True)]
    psum x1 -> x0, waiting for transfers between devices: 37.8 us -> none  [shards(): total_b, total_db = lax.psum((local_b, local_db), 'view')]
    pallas_call x0 -> x4, Pallas kernels: none -> 35.5 us  [run(): pl.pallas_call(body, out_shape=jax.ShapeDtypeStruct(shape, dtype), in_spe...]
    all_to_all x0 -> x1, blocking collectives: none -> 19.3 us  [shards(): lax.all_to_all(summed.reshape(devices, groups // devices, width), ('keys'...]
    scatter x4 -> x0, local copies, waits for them, and re-layouts: 18.1 us -> none  [the longest x2 11.5 us: pack_rows(): sent_payload = jnp.zeros((owners * capacity + 1, payload.shape[1]), paylo...]
  transfers between devices with their start and end apart: 6 -> 4, of which waited for: 2 -> 4; matrix products, arithmetic and copies ran while one was open for 26% -> 0% of each run, Pallas kernels for 0% -> 3%
where the time goes in v1:
time: 134 us
  waiting for transfers between devices  63 us (47%)
  Pallas kernels  35.5 us (26%)
  blocking collectives  19.3 us (14%)
  starting transfers between devices  9.01 us (7%)
  other arithmetic  3 us (2%)
  local copies, waits for them, and re-layouts  2.44 us (2%)
  between operations  1.34 us (1%)
    all_to_all x1, waiting for transfers between devices, shards(): got = lax.all_to_all(sent, 'keys', split_axis=0, concat_axis=0, tiled=True)  46.8 us
    pallas_call x4, Pallas kernels, run(): pl.pallas_call(body, out_shape=jax.ShapeDtypeStruct(shape, dtype), in_spe...  35.5 us
    all_to_all x1, blocking collectives, shards(): lax.all_to_all(summed.reshape(devices, groups // devices, width), ('keys'...  19.3 us
    ppermute x1, waiting for transfers between devices, view_total(): x = x + lax.ppermute(x, 'view', pairs)  12.5 us
    all_to_all x1, starting transfers between devices, shards(): got = lax.all_to_all(sent, 'keys', split_axis=0, concat_axis=0, tiled=True)  7.31 us
  transfers between devices with their start and end apart: 4, of which 4 were waited for; matrix products, arithmetic and copies ran while one was open for 0% of the time, Pallas kernels for 3%

profile of v1, /device:TPU:0, one launch (start us, length us, event | category | flops | bytes accessed | tf_op | source)
XLA Modules:
  0.0 133.6 jit_solution(3711041012801338297)
XLA Ops:
  1.3 10.2 %shard_map.163 = bf16[8,544,256]{2,1,0:T(8,128)(2,1)} custom-call(s32[1]{0:T(128)S(6)} %copy.18.a_count, s32[1]{0:T(128)S(6)} %copy.19.b_count, s32[32,128]{1,0:T(8,128)} %bitcast.13, s32[8,128]{1,0:T(8,128)} %bitcast.19, s32[8,128]{1,0:T(8,128)} %bitcast.20, s32[8,128]{1,0:T(8,128)} %bitcast.21, s32[8,128]{1,0:T(8,128)} %bitcast.22, s32[8,128]{1,0:T(8,128)} %bitcast.23, ...), custom_call_target="tpu_custom_call" | custom-call | tf_op jit(solution)/shard_map/pallas_call | solution.py:201
  11.5 7.3 %all-to-all-start = ((bf16[8,544,256]{2,1,0:T(8,128)(2,1)}), bf16[8,544,256]{2,1,0:T(8,128)(2,1)S(1)}, u32[]{:S(2)}, u32[]{:S(2)}) async-start(bf16[8,544,256]{2,1,0:T(8,128)(2,1)} %shard_map.163), calls=%async_computation | async-start | bytes 4456448 | tf_op jit(solution)/shard_map/all_to_all | solution.py:256
  18.8 4.3 %shard_map.164.local_b = f32[512,256]{1,0:T(8,128)} custom-call(s32[32,128]{1,0:T(8,128)} %bitcast.17, s32[32,128]{1,0:T(8,128)} %bitcast.18, bf16[4096,256]{1,0:T(8,128)(2,1)} %pay_ref.1), custom_call_target="tpu_custom_call" | custom-call | tf_op jit(solution)/shard_map/pallas_call | solution.py:201
  23.0 46.8 %all-to-all-done.got = bf16[8,544,256]{2,1,0:T(8,128)(2,1)S(1)} async-done(((bf16[8,544,256]{2,1,0:T(8,128)(2,1)}), bf16[8,544,256]{2,1,0:T(8,128)(2,1)S(1)}, u32[]{:S(2)}, u32[]{:S(2)}) %all-to-all-start) | async-done | bytes 2228256 | tf_op jit(solution)/shard_map/all_to_all | solution.py:256
  69.8 0.0 copy-start
  69.8 1.4 %copy-done = bf16[8,544,256]{2,1,0:T(8,128)(2,1)} copy-done((bf16[8,544,256]{2,1,0:T(8,128)(2,1)}, bf16[8,544,256]{2,1,0:T(8,128)(2,1)S(1)}, u32[]{:S(2)}) %copy-start) | copy-done | bytes 2228248
  71.2 4.8 %shard_map.165 = f32[512,512]{1,0:T(8,128)} custom-call(f32[512,256]{1,0:T(8,128)} %shard_map.164.local_b, bf16[8,544,256]{2,1,0:T(8,128)(2,1)} %copy-done), custom_call_target="tpu_custom_call" | custom-call | tf_op jit(solution)/shard_map/pallas_call | solution.py:201
  76.0 1.1 constant_dynamic-slice_fusion
  77.1 0.1 collective-permute-start
  77.2 1.9 %collective-permute-done = f32[256,512]{1,0:T(8,128)S(1)} collective-permute-done((f32[256,512]{1,0:T(8,128)S(1)}, f32[256,512]{1,0:T(8,128)S(1)}, u32[]{:S(2)}, u32[]{:S(2)}) %collective-permute-start) | collective-permute-done | bytes 524320 | tf_op jit(solution)/shard_map/ppermute | solution.py:224
  79.1 1.1 dynamic-slice_add_fusion
  80.2 1.6 %collective-permute-start.1 = (f32[256,512]{1,0:T(8,128)S(1)}, f32[256,512]{1,0:T(8,128)S(1)}, u32[]{:S(2)}, u32[]{:S(2)}) collective-permute-start(f32[256,512]{1,0:T(8,128)S(1)} %dynamic-slice_add_fusion), channel_id=1, source_target_pairs={{0,2},{1,3},{2,0},{3,1},{4,6},{5,7},{6,4},{7,5},{8,10},{9,11},{10,... | collective-permute-start | bytes 1572872 | tf_op jit(solution)/shard_map/ppermute | solution.py:227
  81.8 12.5 %collective-permute-done.1 = f32[256,512]{1,0:T(8,128)S(1)} collective-permute-done((f32[256,512]{1,0:T(8,128)S(1)}, f32[256,512]{1,0:T(8,128)S(1)}, u32[]{:S(2)}, u32[]{:S(2)}) %collective-permute-start.1) | collective-permute-done | bytes 524320 | tf_op jit(solution)/shard_map/ppermute | solution.py:227
  94.2 0.1 add.21
  94.3 0.1 collective-permute-start.2
  94.4 1.9 %collective-permute-done.2 = f32[256,512]{1,0:T(8,128)S(1)} collective-permute-done((f32[256,512]{1,0:T(8,128)S(1)}, f32[256,512]{1,0:T(8,128)S(1)}, u32[]{:S(2)}, u32[]{:S(2)}) %collective-permute-start.2) | collective-permute-done | bytes 524320 | tf_op jit(solution)/shard_map/ppermute | solution.py:230
  96.3 1.1 maximum_select_fusion.totals
  97.4 16.2 %shard_map.166 = bf16[1024,256]{1,0:T(8,128)(2,1)} custom-call(s32[32,128]{1,0:T(8,128)} %bitcast.14, s32[32,128]{1,0:T(8,128)} %bitcast.15, s32[32,128]{1,0:T(8,128)} %bitcast.16, bf16[4096,256]{1,0:T(8,128)(2,1)} %a_pay.3, bf16[8,544,256]{2,1,0:T(8,128)(2,1)} %copy-done, f32[512,512]{1,0:T(8,128)} %maximum_select_fusion.totals), custom_call_target="tpu_custom_call" | custom-call | tf_op jit(solution)/shard_map/pallas_call | solution.py:201
  113.6 19.3 %all_to_all.10 = bf16[32,32,256]{2,1,0:T(8,128)(2,1)S(1)} all-to-all(bf16[32,32,256]{2,1,0:T(8,128)(2,1)} %bitcast.12), channel_id=1, replica_groups=mesh['keys'=8,'view'=4] {'keys','view'}, dimensions={0} | all-to-all | bytes 1048576 | tf_op jit(solution)/shard_map/all_to_all | solution.py:275
  132.9 0.7 convert_reduce_fusion
Async XLA Ops:
  11.5 58.4 %all-to-all-start = ((bf16[8,544,256]{2,1,0:T(8,128)(2,1)}), bf16[8,544,256]{2,1,0:T(8,128)(2,1)S(1)}, u32[]{:S(2)}, u32[]{:S(2)}) async-start(bf16[8,544,256]{2,1,0:T(8,128)(2,1)} %shard_map.163), calls=%async_computation | async-start | bytes 4456448 | tf_op jit(solution)/shard_map/all_to_all | solution.py:256
  69.8 1.4 %copy-start = (bf16[8,544,256]{2,1,0:T(8,128)(2,1)}, bf16[8,544,256]{2,1,0:T(8,128)(2,1)S(1)}, u32[]{:S(2)}) copy-start(bf16[8,544,256]{2,1,0:T(8,128)(2,1)S(1)} %all-to-all-done.got) | copy-start | bytes 6684676
  77.1 2.0 %collective-permute-start = (f32[256,512]{1,0:T(8,128)S(1)}, f32[256,512]{1,0:T(8,128)S(1)}, u32[]{:S(2)}, u32[]{:S(2)}) collective-permute-start(f32[256,512]{1,0:T(8,128)S(1)} %constant_dynamic-slice_fusion), channel_id=1, source_target_pairs={{0,1},{1,0},{2,3},{3,2},{4,5},{5,4},{6,7},{7,6},{8,9},{9,8},{10,11... | collective-permute-start | bytes 1572872 | tf_op jit(solution)/shard_map/ppermute | solution.py:224
  80.2 14.0 %collective-permute-start.1 = (f32[256,512]{1,0:T(8,128)S(1)}, f32[256,512]{1,0:T(8,128)S(1)}, u32[]{:S(2)}, u32[]{:S(2)}) collective-permute-start(f32[256,512]{1,0:T(8,128)S(1)} %dynamic-slice_add_fusion), channel_id=1, source_target_pairs={{0,2},{1,3},{2,0},{3,1},{4,6},{5,7},{6,4},{7,5},{8,10},{9,11},{10,... | collective-permute-start | bytes 1572872 | tf_op jit(solution)/shard_map/ppermute | solution.py:227
  94.3 2.0 %collective-permute-start.2 = (f32[256,512]{1,0:T(8,128)S(1)}, f32[256,512]{1,0:T(8,128)S(1)}, u32[]{:S(2)}, u32[]{:S(2)}) collective-permute-start(f32[256,512]{1,0:T(8,128)S(1)} %add.21), channel_id=1, source_target_pairs={{0,1},{1,0},{2,3},{3,2},{4,5},{5,4},{6,7},{7,6},{8,9},{9,8},{10,11... | collective-permute-start | bytes 1572872 | tf_op jit(solution)/shard_map/ppermute | solution.py:230

commit v2 on v1

--- a/solution.py
+++ b/solution.py
@@ -7,11 +7,12 @@
 from jax.experimental.pallas import tpu as pltpu
 from jax.sharding import PartitionSpec as P
 
+
 LANES = 128
 META = 16
 F32 = jnp.float32
 BF16 = jnp.bfloat16
-VMEM_LIMIT = 60 * 1024 * 1024
+VMEM_LIMIT = 20 * 1024 * 1024
 
 
 def row_of(ref, start, count):
@@ -75,9 +76,12 @@
     lax.fori_loop(0, owners, one, 0)
 
 
-def pack_kernel(owners, keys_dev, cap, a_count, b_count, table, a_key, a_group, a_mult, b_key, b_mult, a_pay, b_pay, out):
-    pack_side(owners, keys_dev, cap, 0, table, a_key, a_mult, a_group, a_count[0], a_pay, out)
-    pack_side(owners, keys_dev, cap, cap + META, table, b_key, b_mult, None, b_count[0], b_pay, out)
+def pack_a_kernel(owners, keys_dev, cap, count, table, key, group, mult, pay, out):
+    pack_side(owners, keys_dev, cap, 0, table, key, mult, group, count[0], pay, out)
+
+
+def pack_b_kernel(owners, keys_dev, cap, count, table, key, mult, pay, out):
+    pack_side(owners, keys_dev, cap, 0, table, key, mult, None, count[0], pay, out)
 
 
 def meta_row(got, o, row, cap):
@@ -102,16 +106,13 @@
     lax.fori_loop(0, pay_ref.shape[0] // chunk, one, 0)
 
 
-def delta_kernel(keys_dev, cap, local_b, got, out_ref):
-    base = cap + META
-    width = local_b.shape[1]
-    out_ref[:, :width] = local_b[...]
-    out_ref[:, width:] = jnp.zeros_like(local_b)
+def delta_kernel(keys_dev, cap, got, out_ref):
+    out_ref[...] = jnp.zeros_like(out_ref)
 
     def one(o, carry):
-        slot = meta_row(got, o, base + cap, cap)
+        slot = meta_row(got, o, cap, cap)
         marks = jnp.where(iota((keys_dev, cap), 0) == slot, 1.0, 0.0).astype(BF16)
-        out_ref[:, width:] += dot(marks, got[o, base:base + cap, :])
+        out_ref[...] += dot(marks, got[o, :cap, :])
         return carry
 
     lax.fori_loop(0, got.shape[0], one, 0)
@@ -141,59 +142,71 @@
     return both[:, :width] + both[:, width:]
 
 
-def terms_kernel(
-    cap, a_slot, a_weight, a_group, a_pay, got, totals, out, a_table, d_table, a_terms, d_terms
-):
-    width = a_pay.shape[1]
-    owners = got.shape[0]
+def a_kernel(a_slot, a_weight, a_group, a_pay, db, out, table, terms):
+    count, width = a_pay.shape
     groups = out.shape[0]
-    db = totals[:, width:]
-    a_table[...] = split(db)
-    d_table[...] = split(totals[:, :width] + db)
-    chunk = min(256, a_pay.shape[0])
+    table[...] = split(db[...])
+    chunk = min(256, count)
     lines = chunk // LANES
 
-    def a_one(c, carry):
+    def one(c, carry):
         rows = pl.ds(pl.multiple_of(c * chunk, chunk), chunk)
         picked = gathered(
-            row_of(a_slot, c * lines, lines), row_of(a_weight, c * lines, lines), a_table[...], width
+            row_of(a_slot, c * lines, lines), row_of(a_weight, c * lines, lines), table[...], width
         )
-        a_terms[rows, :] = (a_pay[rows, :].astype(F32) * picked).astype(BF16)
-        return carry
-
-    lax.fori_loop(0, a_pay.shape[0] // chunk, a_one, 0)
-
-    def d_one(o, carry):
-        slot = meta_row(got, o, cap, cap)
-        picked = gathered(slot, jnp.ones_like(slot), d_table[...], width)
-        d_terms[o] = (got[o, :cap, :].astype(F32) * picked).astype(BF16)
-        return carry
-
-    lax.fori_loop(0, owners, d_one, 0)
+        terms[rows, :] = (a_pay[rows, :].astype(F32) * picked).astype(BF16)
+        return carry
+
+    lax.fori_loop(0, count // chunk, one, 0)
 
     block = min(256, groups)
-    span = min(1024, a_pay.shape[0])
+    span = min(1024, count)
     span_lines = span // LANES
 
     def g_one(g, carry):
         first = g * block
         total = jnp.zeros((block, width), F32)
         ids = iota((block, 1), 0) + first
-        for c in range(a_pay.shape[0] // span):
+        for c in range(count // span):
             group = row_of(a_group, c * span_lines, span_lines)
             marks = jnp.where(ids == group, 1.0, 0.0).astype(BF16)
-            total = total + dot(marks, a_terms[c * span:(c + 1) * span, :])
+            total = total + dot(marks, terms[c * span:(c + 1) * span, :])
+        out[pl.ds(pl.multiple_of(first, block), block), :] = total
+        return carry
+
+    lax.fori_loop(0, groups // block, g_one, 0)
+
+
+def d_kernel(cap, got, b, db, partial, out, table, terms):
+    owners, _, width = got.shape
+    groups = out.shape[0]
+    table[...] = split(b[...] + db[...])
+
+    def one(o, carry):
+        slot = meta_row(got, o, cap, cap)
+        picked = gathered(slot, jnp.ones_like(slot), table[...], width)
+        terms[o] = (got[o, :cap, :].astype(F32) * picked).astype(BF16)
+        return carry
+
+    lax.fori_loop(0, owners, one, 0)
+    block = min(256, groups)
+
+    def g_one(g, carry):
+        first = g * block
+        rows = pl.ds(pl.multiple_of(first, block), block)
+        total = partial[rows, :]
+        ids = iota((block, 1), 0) + first
         for o in range(owners):
             group = meta_row(got, o, cap + 2, cap)
             marks = jnp.where(ids == group, 1.0, 0.0).astype(BF16)
-            total = total + dot(marks, d_terms[o])
-        out[pl.ds(pl.multiple_of(first, block), block), :] = total.astype(BF16)
+            total = total + dot(marks, terms[o])
+        out[rows, :] = total.astype(BF16)
         return carry
 
     lax.fori_loop(0, groups // block, g_one, 0)
 
 
-def call(body, shape, dtype, scratch=(), smem=0):
+def call(body, shape, dtype, flops, scratch=(), smem=0):
     def run(*args):
         specs = [pl.BlockSpec(memory_space=pltpu.SMEM)] * smem + [
             pl.BlockSpec(memory_space=pltpu.VMEM)
@@ -205,6 +218,9 @@
             out_specs=pl.BlockSpec(memory_space=pltpu.VMEM),
             scratch_shapes=list(scratch),
             compiler_params=pltpu.CompilerParams(vmem_limit_bytes=VMEM_LIMIT),
+            cost_estimate=pl.CostEstimate(
+                flops=4 * flops, bytes_accessed=sum(x.size * x.dtype.itemsize for x in args), transcendentals=0
+            ),
         )(*args)
 
     return run
@@ -247,31 +263,37 @@
     def lined(x):
         return x.reshape(-1, LANES)
 
-    sent = call(
-        functools.partial(pack_kernel, owners, keys_dev, cap), (owners, 2 * (cap + META), width), BF16, smem=2
-    )(
-        da_count, db_count, lined(key_slot), lined(da_key), lined(da_group), lined(da_mult),
-        lined(db_key), lined(db_mult), da_payload, db_payload,
-    )
-    got = lax.all_to_all(sent, "keys", split_axis=0, concat_axis=0, tiled=True)
-    local_b = call(functools.partial(base_kernel, keys_dev), (keys_dev, width), F32)(
-        lined(b_slot), lined(b_weight), b_payload
-    )
-    local = call(functools.partial(delta_kernel, keys_dev, cap), (keys_dev, 2 * width), F32)(local_b, got)
-    totals = view_total(local, views)
+    packed = (owners, cap + META, width)
+    pack_flops = 2 * owners * cap * delta * width
+    b_sent = call(functools.partial(pack_b_kernel, owners, keys_dev, cap), packed, BF16, pack_flops, smem=1)(
+        db_count, lined(key_slot), lined(db_key), lined(db_mult), db_payload
+    )
+    b_got = lax.all_to_all(b_sent, "keys", split_axis=0, concat_axis=0, tiled=True)
+    a_sent = call(functools.partial(pack_a_kernel, owners, keys_dev, cap), packed, BF16, pack_flops, smem=1)(
+        da_count, lined(key_slot), lined(da_key), lined(da_group), lined(da_mult), da_payload
+    )
+    local_b = call(
+        functools.partial(base_kernel, keys_dev), (keys_dev, width), F32, 2 * keys_dev * b_payload.size
+    )(lined(b_slot), lined(b_weight), b_payload)
+    total_b = view_total(local_b, views)
+    b_got, a_sent, total_b = lax.optimization_barrier((b_got, a_sent, total_b))
+    a_got = lax.all_to_all(a_sent, "keys", split_axis=0, concat_axis=0, tiled=True)
+    local_db = call(
+        functools.partial(delta_kernel, keys_dev, cap), (keys_dev, width), F32, 2 * keys_dev * owners * cap * width
+    )(b_got)
+    total_db = view_total(local_db, views)
+    table = pltpu.VMEM((keys_dev, 2 * width), BF16)
+    a_flops = (4 * keys_dev + 2 * groups) * a_payload.size
+    partial = call(
+        a_kernel, (groups, width), F32, a_flops, scratch=[table, pltpu.VMEM(a_payload.shape, BF16)]
+    )(lined(a_slot), lined(a_weight), lined(a_group), a_payload, total_db)
     summed = call(
-        functools.partial(terms_kernel, cap),
+        functools.partial(d_kernel, cap),
         (groups, width),
         BF16,
-        scratch=[
-            pltpu.VMEM((keys_dev, 2 * width), BF16),
-            pltpu.VMEM((keys_dev, 2 * width), BF16),
-            pltpu.VMEM(a_payload.shape, BF16),
-            pltpu.VMEM((owners, cap, width), BF16),
-        ],
-    )(
-        lined(a_slot), lined(a_weight), lined(a_group), a_payload, got, totals
-    )
+        (4 * keys_dev + 2 * groups) * owners * cap * width,
+        scratch=[table, pltpu.VMEM((owners, cap, width), BF16)],
+    )(a_got, total_b, total_db, partial)
     pieces = lax.all_to_all(
         summed.reshape(devices, groups // devices, width), ("keys", "view"), split_axis=0, concat_axis=0, tiled=True
     )

time: 134 us -> 112 us (0.84)
  waiting for transfers between devices: 63 us -> 42.2 us
  Pallas kernels: 35.5 us -> 26.9 us
  starting transfers between devices: 9.01 us -> 14.5 us
  local copies, waits for them, and re-layouts: 2.44 us -> 6.41 us
  other arithmetic: 3 us -> 0.92 us
    all_to_all x1 -> x2, waiting for transfers between devices: 46.8 us -> 26.1 us  [the longest x1 17.6 us: shards(): lax.all_to_all(a_sent, 'keys', split_axis=0, concat_axis=0, tiled=True)]
    pallas_call x4 -> x6, Pallas kernels: 35.5 us -> 26.9 us  [run(): pl.pallas_call(body, out_shape=jax.ShapeDtypeStruct(shape, dtype), in_spe...]
    unnamed x2 -> x32, local copies, waits for them, and re-layouts: 1.37 us -> 6.35 us
    all_to_all x1 -> x2, starting transfers between devices: 7.31 us -> 11.1 us  [the longest x1 7.44 us: shards(): lax.all_to_all(b_sent, 'keys', split_axis=0, concat_axis=0, tiled=True)]
    ppermute x1 -> x2, waiting for transfers between devices: 1.89 us -> 0.01 us  [view_total(): other = lax.ppermute(x, 'view', pairs)]
    ppermute x1 -> x2, starting transfers between devices: 1.56 us -> 3.11 us  [view_total(): x = x + lax.ppermute(x, 'view', pairs)]
    ppermute x1 -> x2, waiting for transfers between devices: 1.89 us -> 3.04 us  [view_total(): x = keep + lax.ppermute(give, 'view', pairs)]
    ppermute x1 -> x2, waiting for transfers between devices: 12.5 us -> 13.1 us  [view_total(): x = x + lax.ppermute(x, 'view', pairs)]
  transfers between devices with their start and end apart: 4 -> 8, of which waited for: 4 -> 6; matrix products, arithmetic and copies ran while one was open for 0% -> 0% of each run, Pallas kernels for 3% -> 14%
where the time goes in v2:
time: 112 us
  waiting for transfers between devices  42.2 us (38%)
  Pallas kernels  26.9 us (24%)
  blocking collectives  19 us (17%)
  starting transfers between devices  14.5 us (13%)
  local copies, waits for them, and re-layouts  6.41 us (6%)
  between operations  1.6 us (1%)
    pallas_call x6, Pallas kernels, run(): pl.pallas_call(body, out_shape=jax.ShapeDtypeStruct(shape, dtype), in_spe...  26.9 us
    all_to_all x1, blocking collectives, shards(): lax.all_to_all(summed.reshape(devices, groups // devices, width), ('keys'...  19 us
    all_to_all x1, waiting for transfers between devices, shards(): lax.all_to_all(a_sent, 'keys', split_axis=0, concat_axis=0, tiled=True)  17.6 us
    ppermute x2, waiting for transfers between devices, view_total(): x = x + lax.ppermute(x, 'view', pairs)  13.1 us
    all_to_all x1, waiting for transfers between devices, shards(): lax.all_to_all(b_sent, 'keys', split_axis=0, concat_axis=0, tiled=True)  8.59 us
    all_to_all x1, starting transfers between devices, shards(): lax.all_to_all(b_sent, 'keys', split_axis=0, concat_axis=0, tiled=True)  7.44 us
    unnamed x32, local copies, waits for them, and re-layouts  6.35 us
    all_to_all x1, starting transfers between devices, shards(): lax.all_to_all(a_sent, 'keys', split_axis=0, concat_axis=0, tiled=True)  3.65 us
  transfers between devices with their start and end apart: 8, of which 6 were waited for; matrix products, arithmetic and copies ran while one was open for 0% of the time, Pallas kernels for 14%

profile of v2, /device:TPU:0, one launch (start us, length us, event | category | flops | bytes accessed | tf_op | source)
XLA Modules:
  0.0 111.6 jit_solution(16374955431421467806)
XLA Ops:
  0.7 1.0 copy-done.2
  1.7 0.7 copy-done.6
  2.4 0.7 copy-done.11
  3.1 0.7 copy-done.12
  3.8 4.7 %shard_map.163 = bf16[8,272,256]{2,1,0:T(8,128)(2,1)} custom-call(s32[1]{0:T(128)S(6)} %copy.19.count, s32[32,128]{1,0:T(8,128)S(1)} %bitcast.15, s32[8,128]{1,0:T(8,128)S(1)} %bitcast.20, s32[8,128]{1,0:T(8,128)S(1)} %bitcast.21, bf16[1024,256]{1,0:T(8,128)(2,1)S(1)} %copy-done.2), custom_call_target="tpu_custom_call" | custom-call | flops 4294967296 | bytes 548868 | tf_op jit(solution)/shard_map/pallas_call | solution.py:214
  8.5 7.4 %all-to-all-start = ((bf16[8,272,256]{2,1,0:T(8,128)(2,1)}), bf16[8,272,256]{2,1,0:T(8,128)(2,1)S(1)}, u32[]{:S(2)}, u32[]{:S(2)}) async-start(bf16[8,272,256]{2,1,0:T(8,128)(2,1)} %shard_map.163), calls=%async_computation | async-start | bytes 2228224 | tf_op jit(solution)/shard_map/all_to_all | solution.py:271
  16.0 1.6 %copy-done = bf16[4096,256]{1,0:T(8,128)(2,1)S(1)} copy-done((bf16[4096,256]{1,0:T(8,128)(2,1)S(1)}, bf16[4096,256]{1,0:T(8,128)(2,1)}, u32[]{:S(2)}) %copy-start) | copy-done | bytes 2097176
  17.6 1.8 %shard_map.165 = f32[512,256]{1,0:T(8,128)S(1)} custom-call(s32[32,128]{1,0:T(8,128)S(1)} %bitcast.13, s32[32,128]{1,0:T(8,128)S(1)} %bitcast.14, bf16[4096,256]{1,0:T(8,128)(2,1)S(1)} %copy-done), custom_call_target="tpu_custom_call" | custom-call | flops 4294967296 | bytes 2129920 | tf_op jit(solution)/shard_map/pallas_call | solution.py:214
  19.6 1.5 %collective-permute-done = f32[256,256]{1,0:T(8,128)S(1)} collective-permute-done((f32[256,256]{1,0:T(8,128)S(1)}, f32[256,256]{1,0:T(8,128)S(1)}, u32[]{:S(2)}, u32[]{:S(2)}) %collective-permute-start) | collective-permute-done | bytes 262176 | tf_op jit(solution)/shard_map/ppermute | solution.py:240
  21.1 1.6 %collective-permute-start.1 = (f32[256,256]{1,0:T(8,128)S(1)}, f32[256,256]{1,0:T(8,128)S(1)}, u32[]{:S(2)}, u32[]{:S(2)}) collective-permute-start(f32[256,256]{1,0:T(8,128)S(1)} %dynamic-slice_add_fusion.1), channel_id=1, source_target_pairs={{0,2},{1,3},{2,0},{3,1},{4,6},{5,7},{6,4},{7,5},{8,10},{9,11},{10,... | collective-permute-start | bytes 786440 | tf_op jit(solution)/shard_map/ppermute | solution.py:243
  23.3 6.2 %collective-permute-done.1 = f32[256,256]{1,0:T(8,128)S(1)} collective-permute-done((f32[256,256]{1,0:T(8,128)S(1)}, f32[256,256]{1,0:T(8,128)S(1)}, u32[]{:S(2)}, u32[]{:S(2)}) %collective-permute-start.1) | collective-permute-done | bytes 262176 | tf_op jit(solution)/shard_map/ppermute | solution.py:243
  29.7 4.8 %shard_map.164 = bf16[8,272,256]{2,1,0:T(8,128)(2,1)} custom-call(s32[1]{0:T(128)S(6)} %copy.18.count, s32[32,128]{1,0:T(8,128)S(1)} %bitcast.16, s32[8,128]{1,0:T(8,128)S(1)} %bitcast.22, s32[8,128]{1,0:T(8,128)S(1)} %bitcast.23, s32[8,128]{1,0:T(8,128)S(1)} %bitcast.24, bf16[1024,256]{1,0:T(8,128)(2,1)S(1)} %copy-done.3), custom_call_target="tpu_custom_call" | custom-call | flops 4294967296 | bytes 552964 | tf_op jit(solution)/shard_map/pallas_call | solution.py:214
  34.5 8.6 %all-to-all-done.got = bf16[8,272,256]{2,1,0:T(8,128)(2,1)S(1)} async-done(((bf16[8,272,256]{2,1,0:T(8,128)(2,1)}), bf16[8,272,256]{2,1,0:T(8,128)(2,1)S(1)}, u32[]{:S(2)}, u32[]{:S(2)}) %all-to-all-start) | async-done | bytes 1114144 | tf_op jit(solution)/shard_map/all_to_all | solution.py:271
  43.1 2.0 %shard_map.166 = f32[512,256]{1,0:T(8,128)S(1)} custom-call(bf16[8,272,256]{2,1,0:T(8,128)(2,1)S(1)} %all-to-all-done.got), custom_call_target="tpu_custom_call" | custom-call | flops 2147483648 | bytes 1114112 | tf_op jit(solution)/shard_map/pallas_call | solution.py:214
  45.3 1.5 %collective-permute-done.3 = f32[256,256]{1,0:T(8,128)S(1)} collective-permute-done((f32[256,256]{1,0:T(8,128)S(1)}, f32[256,256]{1,0:T(8,128)S(1)}, u32[]{:S(2)}, u32[]{:S(2)}) %collective-permute-start.3) | collective-permute-done | bytes 262176 | tf_op jit(solution)/shard_map/ppermute | solution.py:240
  46.8 1.6 %collective-permute-start.4 = (f32[256,256]{1,0:T(8,128)S(1)}, f32[256,256]{1,0:T(8,128)S(1)}, u32[]{:S(2)}, u32[]{:S(2)}) collective-permute-start(f32[256,256]{1,0:T(8,128)S(1)} %dynamic-slice_add_fusion), channel_id=1, source_target_pairs={{0,2},{1,3},{2,0},{3,1},{4,6},{5,7},{6,4},{7,5},{8,10},{9,11},{10,... | collective-permute-start | bytes 786440 | tf_op jit(solution)/shard_map/ppermute | solution.py:243
  48.4 6.9 %collective-permute-done.4 = f32[256,256]{1,0:T(8,128)S(1)} collective-permute-done((f32[256,256]{1,0:T(8,128)S(1)}, f32[256,256]{1,0:T(8,128)S(1)}, u32[]{:S(2)}, u32[]{:S(2)}) %collective-permute-start.4) | collective-permute-done | bytes 262176 | tf_op jit(solution)/shard_map/ppermute | solution.py:243
  55.4 3.6 %all-to-all-start.1 = ((bf16[8,272,256]{2,1,0:T(8,128)(2,1)}), bf16[8,272,256]{2,1,0:T(8,128)(2,1)S(1)}, u32[]{:S(2)}, u32[]{:S(2)}) async-start(bf16[8,272,256]{2,1,0:T(8,128)(2,1)} %shard_map.164), calls=%async_computation.1 | async-start | bytes 2228224 | tf_op jit(solution)/shard_map/all_to_all | solution.py:280
  59.1 1.6 %copy-done.1 = bf16[4096,256]{1,0:T(8,128)(2,1)S(1)} copy-done((bf16[4096,256]{1,0:T(8,128)(2,1)S(1)}, bf16[4096,256]{1,0:T(8,128)(2,1)}, u32[]{:S(2)}) %copy-start.1) | copy-done | bytes 2097176
  60.7 8.7 %shard_map.167.partial = f32[1024,256]{1,0:T(8,128)S(1)} custom-call(s32[32,128]{1,0:T(8,128)S(1)} %bitcast.17, s32[32,128]{1,0:T(8,128)S(1)} %bitcast.18, s32[32,128]{1,0:T(8,128)S(1)} %bitcast.19, bf16[4096,256]{1,0:T(8,128)(2,1)S(1)} %copy-done.1, f32[512,256]{1,0:T(8,128)S(1)} %maximum_select_fusion.1.db), custom_call_target="tpu_custom_call" | custom-call | flops 17179869184 | bytes 2670592 | tf_op jit(solution)/shard_map/pallas_call | solution.py:214
  69.4 17.6 %all-to-all-done.1.got = bf16[8,272,256]{2,1,0:T(8,128)(2,1)S(1)} async-done(((bf16[8,272,256]{2,1,0:T(8,128)(2,1)}), bf16[8,272,256]{2,1,0:T(8,128)(2,1)S(1)}, u32[]{:S(2)}, u32[]{:S(2)}) %all-to-all-start.1) | async-done | bytes 1114144 | tf_op jit(solution)/shard_map/all_to_all | solution.py:280
  87.0 4.8 %shard_map.168 = bf16[1024,256]{1,0:T(8,128)(2,1)S(1)} custom-call(bf16[8,272,256]{2,1,0:T(8,128)(2,1)S(1)} %all-to-all-done.1.got, f32[512,256]{1,0:T(8,128)S(1)} %maximum_select_fusion.b, f32[512,256]{1,0:T(8,128)S(1)} %maximum_select_fusion.1.db, f32[1024,256]{1,0:T(8,128)S(1)} %shard_map.167.partial), custom_call_target="tpu_custom_call" | custom-call | flops 8589934592 | bytes 3211264 | tf_op jit(solution)/shard_map/pallas_call | solution.py:214
  91.8 19.0 %all_to_all.15 = bf16[32,32,256]{2,1,0:T(8,128)(2,1)S(1)} all-to-all(bf16[32,32,256]{2,1,0:T(8,128)(2,1)S(1)} %bitcast.12), channel_id=1, replica_groups=mesh['keys'=8,'view'=4] {'keys','view'}, dimensions={0} | all-to-all | bytes 1048576 | tf_op jit(solution)/shard_map/all_to_all | solution.py:297
  110.9 0.7 convert_reduce_fusion
  (40 shorter events, 0.6 us)
Async XLA Ops:
  0.7 1.0 copy-start.2
  1.7 0.7 copy-start.6
  2.4 0.7 copy-start.11
  3.1 0.7 copy-start.12
  8.5 7.4 %copy-start.4 = (s32[4096]{0:T(1024)S(1)}, s32[4096]{0:T(1024)}, u32[]{:S(2)}) copy-start(s32[4096]{0:T(1024)} %param.22) | copy-start | bytes 49156
  8.5 7.5 %copy-start.5 = (s32[4096]{0:T(1024)S(1)}, s32[4096]{0:T(1024)}, u32[]{:S(2)}) copy-start(s32[4096]{0:T(1024)} %param.23) | copy-start | bytes 49156
  8.5 34.6 %all-to-all-start = ((bf16[8,272,256]{2,1,0:T(8,128)(2,1)}), bf16[8,272,256]{2,1,0:T(8,128)(2,1)S(1)}, u32[]{:S(2)}, u32[]{:S(2)}) async-start(bf16[8,272,256]{2,1,0:T(8,128)(2,1)} %shard_map.163), calls=%async_computation | async-start | bytes 2228224 | tf_op jit(solution)/shard_map/all_to_all | solution.py:271
  16.0 1.6 %copy-start = (bf16[4096,256]{1,0:T(8,128)(2,1)S(1)}, bf16[4096,256]{1,0:T(8,128)(2,1)}, u32[]{:S(2)}) copy-start(bf16[4096,256]{1,0:T(8,128)(2,1)} %pay_ref.1) | copy-start | bytes 6291460
  19.4 10.3 %copy-start.3 = (bf16[1024,256]{1,0:T(8,128)(2,1)S(1)}, bf16[1024,256]{1,0:T(8,128)(2,1)}, u32[]{:S(2)}) copy-start(bf16[1024,256]{1,0:T(8,128)(2,1)} %pay.3) | copy-start | bytes 1572868
  19.4 10.3 %copy-start.7 = (s32[4096]{0:T(1024)S(1)}, s32[4096]{0:T(1024)}, u32[]{:S(2)}) copy-start(s32[4096]{0:T(1024)} %param.17) | copy-start | bytes 49156
  19.4 10.3 %copy-start.13 = (s32[1024]{0:T(1024)S(1)}, s32[1024]{0:T(1024)}, u32[]{:S(2)}) copy-start(s32[1024]{0:T(1024)} %param.25) | copy-start | bytes 12292
  19.4 10.3 %copy-start.14 = (s32[1024]{0:T(1024)S(1)}, s32[1024]{0:T(1024)}, u32[]{:S(2)}) copy-start(s32[1024]{0:T(1024)} %param.26) | copy-start | bytes 12292
  19.4 10.3 %copy-start.15 = (s32[1024]{0:T(1024)S(1)}, s32[1024]{0:T(1024)}, u32[]{:S(2)}) copy-start(s32[1024]{0:T(1024)} %param.27) | copy-start | bytes 12292
  19.5 1.6 %collective-permute-start = (f32[256,256]{1,0:T(8,128)S(1)}, f32[256,256]{1,0:T(8,128)S(1)}, u32[]{:S(2)}, u32[]{:S(2)}) collective-permute-start(f32[256,256]{1,0:T(8,128)S(1)} %constant_dynamic-slice_fusion.1), channel_id=1, source_target_pairs={{0,1},{1,0},{2,3},{3,2},{4,5},{5,4},{6,7},{7,6},{8,9},{9,8},{10,11... | collective-permute-start | bytes 786440 | tf_op jit(solution)/shard_map/ppermute | solution.py:240
  21.1 8.4 %collective-permute-start.1 = (f32[256,256]{1,0:T(8,128)S(1)}, f32[256,256]{1,0:T(8,128)S(1)}, u32[]{:S(2)}, u32[]{:S(2)}) collective-permute-start(f32[256,256]{1,0:T(8,128)S(1)} %dynamic-slice_add_fusion.1), channel_id=1, source_target_pairs={{0,2},{1,3},{2,0},{3,1},{4,6},{5,7},{6,4},{7,5},{8,10},{9,11},{10,... | collective-permute-start | bytes 786440 | tf_op jit(solution)/shard_map/ppermute | solution.py:243
  29.6 4.9 %collective-permute-start.2 = (f32[256,256]{1,0:T(8,128)S(1)}, f32[256,256]{1,0:T(8,128)S(1)}, u32[]{:S(2)}, u32[]{:S(2)}) collective-permute-start(f32[256,256]{1,0:T(8,128)S(1)} %add.30), channel_id=1, source_target_pairs={{0,1},{1,0},{2,3},{3,2},{4,5},{5,4},{6,7},{7,6},{8,9},{9,8},{10,11... | collective-permute-start | bytes 786440 | tf_op jit(solution)/shard_map/ppermute | solution.py:246
  45.2 1.6 %collective-permute-start.3 = (f32[256,256]{1,0:T(8,128)S(1)}, f32[256,256]{1,0:T(8,128)S(1)}, u32[]{:S(2)}, u32[]{:S(2)}) collective-permute-start(f32[256,256]{1,0:T(8,128)S(1)} %constant_dynamic-slice_fusion), channel_id=1, source_target_pairs={{0,1},{1,0},{2,3},{3,2},{4,5},{5,4},{6,7},{7,6},{8,9},{9,8},{10,11... | collective-permute-start | bytes 786440 | tf_op jit(solution)/shard_map/ppermute | solution.py:240
  46.8 8.4 %collective-permute-start.4 = (f32[256,256]{1,0:T(8,128)S(1)}, f32[256,256]{1,0:T(8,128)S(1)}, u32[]{:S(2)}, u32[]{:S(2)}) collective-permute-start(f32[256,256]{1,0:T(8,128)S(1)} %dynamic-slice_add_fusion), channel_id=1, source_target_pairs={{0,2},{1,3},{2,0},{3,1},{4,6},{5,7},{6,4},{7,5},{8,10},{9,11},{10,... | collective-permute-start | bytes 786440 | tf_op jit(solution)/shard_map/ppermute | solution.py:243
  55.3 3.8 %copy-start.8 = (s32[4096]{0:T(1024)S(1)}, s32[4096]{0:T(1024)}, u32[]{:S(2)}) copy-start(s32[4096]{0:T(1024)} %param.18) | copy-start | bytes 49156
  55.3 3.8 %copy-start.9 = (s32[4096]{0:T(1024)S(1)}, s32[4096]{0:T(1024)}, u32[]{:S(2)}) copy-start(s32[4096]{0:T(1024)} %param.20) | copy-start | bytes 49156
  55.3 3.8 %copy-start.10 = (s32[4096]{0:T(1024)S(1)}, s32[4096]{0:T(1024)}, u32[]{:S(2)}) copy-start(s32[4096]{0:T(1024)} %param.19) | copy-start | bytes 49156
  55.3 3.7 %collective-permute-start.5 = (f32[256,256]{1,0:T(8,128)S(1)}, f32[256,256]{1,0:T(8,128)S(1)}, u32[]{:S(2)}, u32[]{:S(2)}) collective-permute-start(f32[256,256]{1,0:T(8,128)S(1)} %add.32), channel_id=1, source_target_pairs={{0,1},{1,0},{2,3},{3,2},{4,5},{5,4},{6,7},{7,6},{8,9},{9,8},{10,11... | collective-permute-start | bytes 786440 | tf_op jit(solution)/shard_map/ppermute | solution.py:246
  55.4 31.6 %all-to-all-start.1 = ((bf16[8,272,256]{2,1,0:T(8,128)(2,1)}), bf16[8,272,256]{2,1,0:T(8,128)(2,1)S(1)}, u32[]{:S(2)}, u32[]{:S(2)}) async-start(bf16[8,272,256]{2,1,0:T(8,128)(2,1)} %shard_map.164), calls=%async_computation.1 | async-start | bytes 2228224 | tf_op jit(solution)/shard_map/all_to_all | solution.py:280
  59.1 1.6 %copy-start.1 = (bf16[4096,256]{1,0:T(8,128)(2,1)S(1)}, bf16[4096,256]{1,0:T(8,128)(2,1)}, u32[]{:S(2)}) copy-start(bf16[4096,256]{1,0:T(8,128)(2,1)} %a_pay.1) | copy-start | bytes 6291460

commit v3 on v2

--- a/solution.py
+++ b/solution.py
@@ -9,10 +9,11 @@
 
 
 LANES = 128
-META = 16
+META = 8
 F32 = jnp.float32
 BF16 = jnp.bfloat16
-VMEM_LIMIT = 20 * 1024 * 1024
+VMEM_LIMIT = 16 * 1024 * 1024
+WHOLE_LIMIT = 60 * 1024 * 1024
 
 
 def row_of(ref, start, count):
@@ -142,7 +143,19 @@
     return both[:, :width] + both[:, width:]
 
 
-def a_kernel(a_slot, a_weight, a_group, a_pay, db, out, table, terms):
+def group_ids(first, block, groups, owners, views):
+    per_view = groups // views
+    held = per_view // owners
+    place = first // per_view
+    at = iota((block, 1), 0) + (first - place * per_view)
+    bits = views.bit_length() - 1
+    rel = sum(((place >> b) & 1) << (bits - 1 - b) for b in range(bits))
+    view = rel ^ lax.axis_index("view")
+    owner = at // held
+    return (owner * views + view) * held + (at - owner * held)
+
+
+def a_kernel(owners, views, a_slot, a_weight, a_group, a_pay, db, out, table, terms):
     count, width = a_pay.shape
     groups = out.shape[0]
     table[...] = split(db[...])
@@ -159,14 +172,14 @@
 
     lax.fori_loop(0, count // chunk, one, 0)
 
-    block = min(256, groups)
+    block = min(256, groups // views)
     span = min(1024, count)
     span_lines = span // LANES
 
     def g_one(g, carry):
         first = g * block
         total = jnp.zeros((block, width), F32)
-        ids = iota((block, 1), 0) + first
+        ids = group_ids(first, block, groups, owners, views)
         for c in range(count // span):
             group = row_of(a_group, c * span_lines, span_lines)
             marks = jnp.where(ids == group, 1.0, 0.0).astype(BF16)
@@ -177,9 +190,9 @@
     lax.fori_loop(0, groups // block, g_one, 0)
 
 
-def d_kernel(cap, got, b, db, partial, out, table, terms):
+def d_kernel(cap, views, got, b, db, partial, keep, give, table, terms):
     owners, _, width = got.shape
-    groups = out.shape[0]
+    groups = partial.shape[0]
     table[...] = split(b[...] + db[...])
 
     def one(o, carry):
@@ -189,39 +202,51 @@
         return carry
 
     lax.fori_loop(0, owners, one, 0)
-    block = min(256, groups)
-
-    def g_one(g, carry):
+    block = min(256, groups // views)
+
+    def g_one(g):
         first = g * block
         rows = pl.ds(pl.multiple_of(first, block), block)
         total = partial[rows, :]
-        ids = iota((block, 1), 0) + first
+        ids = group_ids(first, block, groups, owners, views)
         for o in range(owners):
             group = meta_row(got, o, cap + 2, cap)
             marks = jnp.where(ids == group, 1.0, 0.0).astype(BF16)
             total = total + dot(marks, terms[o])
-        out[rows, :] = total.astype(BF16)
-        return carry
-
-    lax.fori_loop(0, groups // block, g_one, 0)
-
-
-def call(body, shape, dtype, flops, scratch=(), smem=0):
+        return first, total
+
+    def k_one(g, carry):
+        first, total = g_one(g)
+        keep[pl.ds(pl.multiple_of(first, block), block), :] = total
+        return carry
+
+    def s_one(g, carry):
+        first, total = g_one(g + blocks)
+        give[pl.ds(pl.multiple_of(first - groups // 2, block), block), :] = total
+        return carry
+
+    blocks = groups // 2 // block
+    lax.fori_loop(0, blocks, s_one, 0)
+    lax.fori_loop(0, blocks, k_one, 0)
+
+
+def call(body, shape, dtype, flops, scratch=(), smem=0, outs=1, limit=VMEM_LIMIT):
     def run(*args):
         specs = [pl.BlockSpec(memory_space=pltpu.SMEM)] * smem + [
             pl.BlockSpec(memory_space=pltpu.VMEM)
         ] * (len(args) - smem)
-        return pl.pallas_call(
+        made = pl.pallas_call(
             body,
-            out_shape=jax.ShapeDtypeStruct(shape, dtype),
+            out_shape=[jax.ShapeDtypeStruct(shape, dtype)] * outs,
             in_specs=specs,
-            out_specs=pl.BlockSpec(memory_space=pltpu.VMEM),
+            out_specs=[pl.BlockSpec(memory_space=pltpu.VMEM)] * outs,
             scratch_shapes=list(scratch),
-            compiler_params=pltpu.CompilerParams(vmem_limit_bytes=VMEM_LIMIT),
+            compiler_params=pltpu.CompilerParams(vmem_limit_bytes=limit),
             cost_estimate=pl.CostEstimate(
                 flops=4 * flops, bytes_accessed=sum(x.size * x.dtype.itemsize for x in args), transcendentals=0
             ),
         )(*args)
+        return made if outs > 1 else made[0]
 
     return run
 
@@ -253,7 +278,6 @@
     da_key, da_group, da_mult, da_payload, da_count, db_key, db_mult, db_payload, db_count,
 ):
     owners, views = lax.axis_size("keys"), lax.axis_size("view")
-    devices = owners * views
     width = a_payload.shape[1]
     keys_dev = key_slot.shape[0] // owners
     delta = da_payload.shape[0]
@@ -265,7 +289,7 @@
 
     packed = (owners, cap + META, width)
     pack_flops = 2 * owners * cap * delta * width
-    b_sent = call(functools.partial(pack_b_kernel, owners, keys_dev, cap), packed, BF16, pack_flops, smem=1)(
+    b_sent = call(functools.partial(pack_b_kernel, owners, keys_dev, cap), packed, BF16, pack_flops, smem=1, limit=WHOLE_LIMIT)(
         db_count, lined(key_slot), lined(db_key), lined(db_mult), db_payload
     )
     b_got = lax.all_to_all(b_sent, "keys", split_axis=0, concat_axis=0, tiled=True)
@@ -285,17 +309,25 @@
     table = pltpu.VMEM((keys_dev, 2 * width), BF16)
     a_flops = (4 * keys_dev + 2 * groups) * a_payload.size
     partial = call(
-        a_kernel, (groups, width), F32, a_flops, scratch=[table, pltpu.VMEM(a_payload.shape, BF16)]
+        functools.partial(a_kernel, owners, views), (groups, width), F32, a_flops, scratch=[table, pltpu.VMEM(a_payload.shape, BF16)]
     )(lined(a_slot), lined(a_weight), lined(a_group), a_payload, total_db)
-    summed = call(
-        functools.partial(d_kernel, cap),
-        (groups, width),
-        BF16,
+    keep, give = call(
+        functools.partial(d_kernel, cap, views),
+        (groups // 2, width),
+        F32,
         (4 * keys_dev + 2 * groups) * owners * cap * width,
         scratch=[table, pltpu.VMEM((owners, cap, width), BF16)],
+        outs=2,
     )(a_got, total_b, total_db, partial)
+    total = keep + lax.ppermute(give, "view", [(i, i ^ 1) for i in range(views)])
+    bit = 2
+    while bit < views:
+        half = total.shape[0] // 2
+        given = total[half:].astype(BF16)
+        total = total[:half] + lax.ppermute(given, "view", [(i, i ^ bit) for i in range(views)]).astype(F32)
+        bit *= 2
     pieces = lax.all_to_all(
-        summed.reshape(devices, groups // devices, width), ("keys", "view"), split_axis=0, concat_axis=0, tiled=True
+        total.astype(BF16).reshape(owners, -1, width), "keys", split_axis=0, concat_axis=0, tiled=True
     )
     return jnp.sum(pieces.astype(F32), axis=0)
 

time: 112 us -> 108 us (0.964)
  blocking collectives: 19 us -> 10.8 us
  waiting for transfers between devices: 42.2 us -> 46.6 us
  local copies, waits for them, and re-layouts: 6.41 us -> 3.3 us
  starting transfers between devices: 14.5 us -> 16.1 us
  Pallas kernels: 26.9 us -> 28.3 us
    all_to_all x1, blocking collectives: 19 us -> 10.8 us  [shards(): lax.all_to_all(total.astype(BF16).reshape(owners, -1, width), 'keys', spl...]
    ppermute x0 -> x2, waiting for transfers between devices: none -> 5.94 us  [the longest x1 4.04 us: shards(): lax.ppermute(given, 'view', [(i, i ^ bit) for i in range(views)])]
    unnamed x32 -> x24, local copies, waits for them, and re-layouts: 6.35 us -> 3.23 us
    ppermute x0 -> x2, starting transfers between devices: none -> 1.63 us  [the longest x1 1.56 us: shards(): lax.ppermute(given, 'view', [(i, i ^ bit) for i in range(views)])]
    pallas_call x6, Pallas kernels: 26.9 us -> 28.3 us  [run(): pl.pallas_call(body, out_shape=[jax.ShapeDtypeStruct(shape, dtype)] * out...]
  transfers between devices with their start and end apart: 8 -> 10, of which waited for: 6 -> 8; matrix products, arithmetic and copies ran while one was open for 0% -> 0% of each run, Pallas kernels for 14% -> 14%
where the time goes in v3:
time: 108 us
  waiting for transfers between devices  46.6 us (43%)
  Pallas kernels  28.3 us (26%)
  starting transfers between devices  16.1 us (15%)
  blocking collectives  10.8 us (10%)
  local copies, waits for them, and re-layouts  3.3 us (3%)
  between operations  1.61 us (1%)
    pallas_call x6, Pallas kernels, run(): pl.pallas_call(body, out_shape=[jax.ShapeDtypeStruct(shape, dtype)] * out...  28.3 us
    all_to_all x1, waiting for transfers between devices, shards(): lax.all_to_all(a_sent, 'keys', split_axis=0, concat_axis=0, tiled=True)  16.7 us
    ppermute x2, waiting for transfers between devices, view_total(): x = x + lax.ppermute(x, 'view', pairs)  13.1 us
    all_to_all x1, blocking collectives, shards(): lax.all_to_all(total.astype(BF16).reshape(owners, -1, width), 'keys', spl...  10.8 us
    all_to_all x1, waiting for transfers between devices, shards(): lax.all_to_all(b_sent, 'keys', split_axis=0, concat_axis=0, tiled=True)  7.92 us
    all_to_all x1, starting transfers between devices, shards(): lax.all_to_all(b_sent, 'keys', split_axis=0, concat_axis=0, tiled=True)  7.44 us
    ppermute x1, waiting for transfers between devices, shards(): lax.ppermute(given, 'view', [(i, i ^ bit) for i in range(views)])  4.04 us
    all_to_all x1, starting transfers between devices, shards(): lax.all_to_all(a_sent, 'keys', split_axis=0, concat_axis=0, tiled=True)  3.65 us
  transfers between devices with their start and end apart: 10, of which 8 were waited for; matrix products, arithmetic and copies ran while one was open for 0% of the time, Pallas kernels for 14%

profile of v3, /device:TPU:0, one launch (start us, length us, event | category | flops | bytes accessed | tf_op | source)
XLA Modules:
  0.0 107.7 jit_solution(4722941690118491702)
XLA Ops:
  0.7 5.8 %shard_map.163 = bf16[8,264,256]{2,1,0:T(8,128)(2,1)} custom-call(s32[1]{0:T(128)S(6)} %copy.19.count, s32[32,128]{1,0:T(8,128)} %bitcast.14, s32[8,128]{1,0:T(8,128)} %bitcast.23, s32[8,128]{1,0:T(8,128)} %bitcast.24, bf16[1024,256]{1,0:T(8,128)(2,1)} %pay.2), custom_call_target="tpu_custom_call" | custom-call | flops 4294967296 | bytes 548868 | tf_op jit(solution)/shard_map/pallas_call | solution.py:238
  6.5 7.4 %all-to-all-start = ((bf16[8,264,256]{2,1,0:T(8,128)(2,1)}), bf16[8,264,256]{2,1,0:T(8,128)(2,1)S(1)}, u32[]{:S(2)}, u32[]{:S(2)}) async-start(bf16[8,264,256]{2,1,0:T(8,128)(2,1)} %shard_map.163), calls=%async_computation | async-start | bytes 2162688 | tf_op jit(solution)/shard_map/all_to_all | solution.py:295
  14.0 1.6 %copy-done = bf16[4096,256]{1,0:T(8,128)(2,1)S(1)} copy-done((bf16[4096,256]{1,0:T(8,128)(2,1)S(1)}, bf16[4096,256]{1,0:T(8,128)(2,1)}, u32[]{:S(2)}) %copy-start) | copy-done | bytes 2097176
  15.5 1.8 %shard_map.165 = f32[512,256]{1,0:T(8,128)S(1)} custom-call(s32[32,128]{1,0:T(8,128)S(1)} %bitcast.12, s32[32,128]{1,0:T(8,128)S(1)} %bitcast.13, bf16[4096,256]{1,0:T(8,128)(2,1)S(1)} %copy-done), custom_call_target="tpu_custom_call" | custom-call | flops 4294967296 | bytes 2129920 | tf_op jit(solution)/shard_map/pallas_call | solution.py:238
  17.4 0.1 collective-permute-start
  17.5 1.5 %collective-permute-done = f32[256,256]{1,0:T(8,128)S(1)} collective-permute-done((f32[256,256]{1,0:T(8,128)S(1)}, f32[256,256]{1,0:T(8,128)S(1)}, u32[]{:S(2)}, u32[]{:S(2)}) %collective-permute-start) | collective-permute-done | bytes 262176 | tf_op jit(solution)/shard_map/ppermute | solution.py:265
  19.1 1.6 %collective-permute-start.1 = (f32[256,256]{1,0:T(8,128)S(1)}, f32[256,256]{1,0:T(8,128)S(1)}, u32[]{:S(2)}, u32[]{:S(2)}) collective-permute-start(f32[256,256]{1,0:T(8,128)S(1)} %dynamic-slice_add_fusion.1), channel_id=1, source_target_pairs={{0,2},{1,3},{2,0},{3,1},{4,6},{5,7},{6,4},{7,5},{8,10},{9,11},{10,... | collective-permute-start | bytes 786440 | tf_op jit(solution)/shard_map/ppermute | solution.py:268
  21.3 6.2 %collective-permute-done.1 = f32[256,256]{1,0:T(8,128)S(1)} collective-permute-done((f32[256,256]{1,0:T(8,128)S(1)}, f32[256,256]{1,0:T(8,128)S(1)}, u32[]{:S(2)}, u32[]{:S(2)}) %collective-permute-start.1) | collective-permute-done | bytes 262176 | tf_op jit(solution)/shard_map/ppermute | solution.py:268
  27.7 4.8 %shard_map.164 = bf16[8,264,256]{2,1,0:T(8,128)(2,1)} custom-call(s32[1]{0:T(128)S(6)} %copy.18.count, s32[32,128]{1,0:T(8,128)S(1)} %bitcast.15, s32[8,128]{1,0:T(8,128)S(1)} %bitcast.19, s32[8,128]{1,0:T(8,128)S(1)} %bitcast.20, s32[8,128]{1,0:T(8,128)S(1)} %bitcast.21, bf16[1024,256]{1,0:T(8,128)(2,1)S(1)} %copy-done.2), custom_call_target="tpu_custom_call" | custom-call | flops 4294967296 | bytes 552964 | tf_op jit(solution)/shard_map/pallas_call | solution.py:238
  32.5 7.9 %all-to-all-done.got = bf16[8,264,256]{2,1,0:T(8,128)(2,1)S(1)} async-done(((bf16[8,264,256]{2,1,0:T(8,128)(2,1)}), bf16[8,264,256]{2,1,0:T(8,128)(2,1)S(1)}, u32[]{:S(2)}, u32[]{:S(2)}) %all-to-all-start) | async-done | bytes 1081376 | tf_op jit(solution)/shard_map/all_to_all | solution.py:295
  40.4 2.0 %shard_map.166 = f32[512,256]{1,0:T(8,128)S(1)} custom-call(bf16[8,264,256]{2,1,0:T(8,128)(2,1)S(1)} %all-to-all-done.got), custom_call_target="tpu_custom_call" | custom-call | flops 2147483648 | bytes 1081344 | tf_op jit(solution)/shard_map/pallas_call | solution.py:238
  42.5 1.5 %collective-permute-done.3 = f32[256,256]{1,0:T(8,128)S(1)} collective-permute-done((f32[256,256]{1,0:T(8,128)S(1)}, f32[256,256]{1,0:T(8,128)S(1)}, u32[]{:S(2)}, u32[]{:S(2)}) %collective-permute-start.3) | collective-permute-done | bytes 262176 | tf_op jit(solution)/shard_map/ppermute | solution.py:265
  44.1 1.6 %collective-permute-start.4 = (f32[256,256]{1,0:T(8,128)S(1)}, f32[256,256]{1,0:T(8,128)S(1)}, u32[]{:S(2)}, u32[]{:S(2)}) collective-permute-start(f32[256,256]{1,0:T(8,128)S(1)} %dynamic-slice_add_fusion), channel_id=1, source_target_pairs={{0,2},{1,3},{2,0},{3,1},{4,6},{5,7},{6,4},{7,5},{8,10},{9,11},{10,... | collective-permute-start | bytes 786440 | tf_op jit(solution)/shard_map/ppermute | solution.py:268
  45.7 6.9 %collective-permute-done.4 = f32[256,256]{1,0:T(8,128)S(1)} collective-permute-done((f32[256,256]{1,0:T(8,128)S(1)}, f32[256,256]{1,0:T(8,128)S(1)}, u32[]{:S(2)}, u32[]{:S(2)}) %collective-permute-start.4) | collective-permute-done | bytes 262176 | tf_op jit(solution)/shard_map/ppermute | solution.py:268
  52.7 3.6 %all-to-all-start.1 = ((bf16[8,264,256]{2,1,0:T(8,128)(2,1)}), bf16[8,264,256]{2,1,0:T(8,128)(2,1)S(1)}, u32[]{:S(2)}, u32[]{:S(2)}) async-start(bf16[8,264,256]{2,1,0:T(8,128)(2,1)} %shard_map.164), calls=%async_computation.1 | async-start | bytes 2162688 | tf_op jit(solution)/shard_map/all_to_all | solution.py:304
  56.4 1.6 %copy-done.1 = bf16[4096,256]{1,0:T(8,128)(2,1)S(1)} copy-done((bf16[4096,256]{1,0:T(8,128)(2,1)S(1)}, bf16[4096,256]{1,0:T(8,128)(2,1)}, u32[]{:S(2)}) %copy-start.1) | copy-done | bytes 2097176
  58.0 8.9 %shard_map.167.partial = f32[1024,256]{1,0:T(8,128)S(1)} custom-call(s32[32,128]{1,0:T(8,128)S(1)} %bitcast.16, s32[32,128]{1,0:T(8,128)S(1)} %bitcast.17, s32[32,128]{1,0:T(8,128)S(1)} %bitcast.18, bf16[4096,256]{1,0:T(8,128)(2,1)S(1)} %copy-done.1, f32[512,256]{1,0:T(8,128)S(1)} %maximum_select_fusion.1.db), custom_call_target="tpu_custom_call" | custom-call | flops 17179869184 | bytes 2670592 | tf_op jit(solution)/shard_map/pallas_call | solution.py:238
  66.9 16.7 %all-to-all-done.1.got = bf16[8,264,256]{2,1,0:T(8,128)(2,1)S(1)} async-done(((bf16[8,264,256]{2,1,0:T(8,128)(2,1)}), bf16[8,264,256]{2,1,0:T(8,128)(2,1)S(1)}, u32[]{:S(2)}, u32[]{:S(2)}) %all-to-all-start.1) | async-done | bytes 1081376 | tf_op jit(solution)/shard_map/all_to_all | solution.py:304
  83.5 5.0 %shard_map.168 = (f32[512,256]{1,0:T(8,128)S(1)}, f32[512,256]{1,0:T(8,128)S(1)}) custom-call(bf16[8,264,256]{2,1,0:T(8,128)(2,1)S(1)} %all-to-all-done.1.got, f32[512,256]{1,0:T(8,128)S(1)} %maximum_select_fusion.b, f32[512,256]{1,0:T(8,128)S(1)} %maximum_select_fusion.1.db, f32[1024,256]{1,0:T(8,128)S(1)} %shard_map.167.partial), custom_call_target="tpu_custom_call" | custom-call | flops 8589934592 | bytes 3178496 | tf_op jit(solution)/shard_map/pallas_call | solution.py:238
  88.6 1.9 %collective-permute-done.6 = f32[512,256]{1,0:T(8,128)S(1)} collective-permute-done((f32[512,256]{1,0:T(8,128)S(1)}, f32[512,256]{1,0:T(8,128)S(1)}, u32[]{:S(2)}, u32[]{:S(2)}) %collective-permute-start.6) | collective-permute-done | bytes 524320 | tf_op jit(solution)/shard_map/ppermute | solution.py:322
  90.6 1.6 %collective-permute-start.7 = (bf16[256,256]{1,0:T(8,128)(2,1)S(1)}, bf16[256,256]{1,0:T(8,128)(2,1)S(1)}, u32[]{:S(2)}, u32[]{:S(2)}) collective-permute-start(bf16[256,256]{1,0:T(8,128)(2,1)S(1)} %slice.15), channel_id=1, source_target_pairs={{0,2},{1,3},{2,0},{3,1},{4,6},{5,7},{6,4},{7,5},{8,10},{9,11},{10,... | collective-permute-start | bytes 393224 | tf_op jit(solution)/shard_map/ppermute | solution.py:327
  92.2 4.0 %collective-permute-done.7 = bf16[256,256]{1,0:T(8,128)(2,1)S(1)} collective-permute-done((bf16[256,256]{1,0:T(8,128)(2,1)S(1)}, bf16[256,256]{1,0:T(8,128)(2,1)S(1)}, u32[]{:S(2)}, u32[]{:S(2)}) %collective-permute-start.7) | collective-permute-done | bytes 131104 | tf_op jit(solution)/shard_map/ppermute | solution.py:327
  96.3 10.8 %all_to_all.15 = bf16[8,32,256]{2,1,0:T(8,128)(2,1)S(1)} all-to-all(bf16[8,32,256]{2,1,0:T(8,128)(2,1)S(1)} %bitcast.22), channel_id=1, replica_groups=mesh['keys'=8,'view'=4] {'keys'}, dimensions={0} | all-to-all | bytes 262144 | tf_op jit(solution)/shard_map/all_to_all | solution.py:329
  107.0 0.6 convert_reduce_fusion
  (39 shorter events, 0.7 us)
Async XLA Ops:
  6.5 7.4 %copy-start.3 = (s32[4096]{0:T(1024)S(1)}, s32[4096]{0:T(1024)}, u32[]{:S(2)}) copy-start(s32[4096]{0:T(1024)} %param.22) | copy-start | bytes 49156
  6.5 7.5 %copy-start.4 = (s32[4096]{0:T(1024)S(1)}, s32[4096]{0:T(1024)}, u32[]{:S(2)}) copy-start(s32[4096]{0:T(1024)} %param.23) | copy-start | bytes 49156
  6.5 33.9 %all-to-all-start = ((bf16[8,264,256]{2,1,0:T(8,128)(2,1)}), bf16[8,264,256]{2,1,0:T(8,128)(2,1)S(1)}, u32[]{:S(2)}, u32[]{:S(2)}) async-start(bf16[8,264,256]{2,1,0:T(8,128)(2,1)} %shard_map.163), calls=%async_computation | async-start | bytes 2162688 | tf_op jit(solution)/shard_map/all_to_all | solution.py:295
  13.9 1.6 %copy-start = (bf16[4096,256]{1,0:T(8,128)(2,1)S(1)}, bf16[4096,256]{1,0:T(8,128)(2,1)}, u32[]{:S(2)}) copy-start(bf16[4096,256]{1,0:T(8,128)(2,1)} %pay_ref.1) | copy-start | bytes 6291460
  17.4 10.3 %copy-start.2 = (bf16[1024,256]{1,0:T(8,128)(2,1)S(1)}, bf16[1024,256]{1,0:T(8,128)(2,1)}, u32[]{:S(2)}) copy-start(bf16[1024,256]{1,0:T(8,128)(2,1)} %pay.3) | copy-start | bytes 1572868
  17.4 10.3 %copy-start.5 = (s32[4096]{0:T(1024)S(1)}, s32[4096]{0:T(1024)}, u32[]{:S(2)}) copy-start(s32[4096]{0:T(1024)} %param.17) | copy-start | bytes 49156
  17.4 10.3 %copy-start.9 = (s32[1024]{0:T(1024)S(1)}, s32[1024]{0:T(1024)}, u32[]{:S(2)}) copy-start(s32[1024]{0:T(1024)} %param.25) | copy-start | bytes 12292
  17.4 10.3 %copy-start.10 = (s32[1024]{0:T(1024)S(1)}, s32[1024]{0:T(1024)}, u32[]{:S(2)}) copy-start(s32[1024]{0:T(1024)} %param.26) | copy-start | bytes 12292
  17.4 10.3 %copy-start.11 = (s32[1024]{0:T(1024)S(1)}, s32[1024]{0:T(1024)}, u32[]{:S(2)}) copy-start(s32[1024]{0:T(1024)} %param.27) | copy-start | bytes 12292
  17.4 1.6 %collective-permute-start = (f32[256,256]{1,0:T(8,128)S(1)}, f32[256,256]{1,0:T(8,128)S(1)}, u32[]{:S(2)}, u32[]{:S(2)}) collective-permute-start(f32[256,256]{1,0:T(8,128)S(1)} %constant_dynamic-slice_fusion.1), channel_id=1, source_target_pairs={{0,1},{1,0},{2,3},{3,2},{4,5},{5,4},{6,7},{7,6},{8,9},{9,8},{10,11... | collective-permute-start | bytes 786440 | tf_op jit(solution)/shard_map/ppermute | solution.py:265
  19.1 8.4 %collective-permute-start.1 = (f32[256,256]{1,0:T(8,128)S(1)}, f32[256,256]{1,0:T(8,128)S(1)}, u32[]{:S(2)}, u32[]{:S(2)}) collective-permute-start(f32[256,256]{1,0:T(8,128)S(1)} %dynamic-slice_add_fusion.1), channel_id=1, source_target_pairs={{0,2},{1,3},{2,0},{3,1},{4,6},{5,7},{6,4},{7,5},{8,10},{9,11},{10,... | collective-permute-start | bytes 786440 | tf_op jit(solution)/shard_map/ppermute | solution.py:268
  27.5 4.9 %collective-permute-start.2 = (f32[256,256]{1,0:T(8,128)S(1)}, f32[256,256]{1,0:T(8,128)S(1)}, u32[]{:S(2)}, u32[]{:S(2)}) collective-permute-start(f32[256,256]{1,0:T(8,128)S(1)} %add.36), channel_id=1, source_target_pairs={{0,1},{1,0},{2,3},{3,2},{4,5},{5,4},{6,7},{7,6},{8,9},{9,8},{10,11... | collective-permute-start | bytes 786440 | tf_op jit(solution)/shard_map/ppermute | solution.py:271
  42.5 1.6 %collective-permute-start.3 = (f32[256,256]{1,0:T(8,128)S(1)}, f32[256,256]{1,0:T(8,128)S(1)}, u32[]{:S(2)}, u32[]{:S(2)}) collective-permute-start(f32[256,256]{1,0:T(8,128)S(1)} %constant_dynamic-slice_fusion), channel_id=1, source_target_pairs={{0,1},{1,0},{2,3},{3,2},{4,5},{5,4},{6,7},{7,6},{8,9},{9,8},{10,11... | collective-permute-start | bytes 786440 | tf_op jit(solution)/shard_map/ppermute | solution.py:265
  44.1 8.4 %collective-permute-start.4 = (f32[256,256]{1,0:T(8,128)S(1)}, f32[256,256]{1,0:T(8,128)S(1)}, u32[]{:S(2)}, u32[]{:S(2)}) collective-permute-start(f32[256,256]{1,0:T(8,128)S(1)} %dynamic-slice_add_fusion), channel_id=1, source_target_pairs={{0,2},{1,3},{2,0},{3,1},{4,6},{5,7},{6,4},{7,5},{8,10},{9,11},{10,... | collective-permute-start | bytes 786440 | tf_op jit(solution)/shard_map/ppermute | solution.py:268
  52.5 3.8 %copy-start.6 = (s32[4096]{0:T(1024)S(1)}, s32[4096]{0:T(1024)}, u32[]{:S(2)}) copy-start(s32[4096]{0:T(1024)} %param.18) | copy-start | bytes 49156
  52.6 3.8 %copy-start.7 = (s32[4096]{0:T(1024)S(1)}, s32[4096]{0:T(1024)}, u32[]{:S(2)}) copy-start(s32[4096]{0:T(1024)} %param.20) | copy-start | bytes 49156
  52.6 3.8 %copy-start.8 = (s32[4096]{0:T(1024)S(1)}, s32[4096]{0:T(1024)}, u32[]{:S(2)}) copy-start(s32[4096]{0:T(1024)} %param.19) | copy-start | bytes 49156
  52.6 3.7 %collective-permute-start.5 = (f32[256,256]{1,0:T(8,128)S(1)}, f32[256,256]{1,0:T(8,128)S(1)}, u32[]{:S(2)}, u32[]{:S(2)}) collective-permute-start(f32[256,256]{1,0:T(8,128)S(1)} %add.38), channel_id=1, source_target_pairs={{0,1},{1,0},{2,3},{3,2},{4,5},{5,4},{6,7},{7,6},{8,9},{9,8},{10,11... | collective-permute-start | bytes 786440 | tf_op jit(solution)/shard_map/ppermute | solution.py:271
  52.7 30.9 %all-to-all-start.1 = ((bf16[8,264,256]{2,1,0:T(8,128)(2,1)}), bf16[8,264,256]{2,1,0:T(8,128)(2,1)S(1)}, u32[]{:S(2)}, u32[]{:S(2)}) async-start(bf16[8,264,256]{2,1,0:T(8,128)(2,1)} %shard_map.164), calls=%async_computation.1 | async-start | bytes 2162688 | tf_op jit(solution)/shard_map/all_to_all | solution.py:304
  56.4 1.6 %copy-start.1 = (bf16[4096,256]{1,0:T(8,128)(2,1)S(1)}, bf16[4096,256]{1,0:T(8,128)(2,1)}, u32[]{:S(2)}) copy-start(bf16[4096,256]{1,0:T(8,128)(2,1)} %a_pay.1) | copy-start | bytes 6291460
  88.5 2.0 %collective-permute-start.6 = (f32[512,256]{1,0:T(8,128)S(1)}, f32[512,256]{1,0:T(8,128)S(1)}, u32[]{:S(2)}, u32[]{:S(2)}) collective-permute-start(f32[512,256]{1,0:T(8,128)S(1)} %get-tuple-element.14), channel_id=1, source_target_pairs={{0,1},{1,0},{2,3},{3,2},{4,5},{5,4},{6,7},{7,6},{8,9},{9,8},{10,11... | collective-permute-start | bytes 1572872 | tf_op jit(solution)/shard_map/ppermute | solution.py:322
  90.6 5.6 %collective-permute-start.7 = (bf16[256,256]{1,0:T(8,128)(2,1)S(1)}, bf16[256,256]{1,0:T(8,128)(2,1)S(1)}, u32[]{:S(2)}, u32[]{:S(2)}) collective-permute-start(bf16[256,256]{1,0:T(8,128)(2,1)S(1)} %slice.15), channel_id=1, source_target_pairs={{0,2},{1,3},{2,0},{3,1},{4,6},{5,7},{6,4},{7,5},{8,10},{9,11},{10,... | collective-permute-start | bytes 393224 | tf_op jit(solution)/shard_map/ppermute | solution.py:327
